TPU v7x, 32 devices: a whole 2x2x4 slice. The times are simulated.
32 devices in a mesh: dp: 2 (over x), mode: 4 (over z), tm: 4 (over y, core).
Axes of the slice: x: 2, y: 2, z: 4, core: 2. Of those that a mesh axis runs over, the one named last changes fastest.
Arguments:
- input_field: float32 [2, 16, 8, 16384], P(None, 'dp', 'mode', 'tm'), parts along dimension 1, may hold values from -6 to 6
- target_field: float32 [2, 16, 8, 16384], P(None, 'dp', 'mode', 'tm'), parts along dimension 1, may hold values from -6 to 6
- margin: float32 [8, 8, 16], P('mode'), may hold values from -0.5 to 0.5
- pair_index: int32 [16, 2], replicated, may hold values from 0 to 7
- mode_beta: float32 [1024, 8, 3], P(None, 'mode'), may hold values from -2 to 2
- segment_kind: int32 [1], replicated, may hold values from 0 to 1023
Outputs:
- field_gradient: float32 [2, 16, 8, 16384], P(None, 'dp', 'mode', 'tm'), parts along dimension 1
There are 2 independent parts, one for each index of `dp`. A program takes and returns all parts, laid end to end along the dimension named above; an argument that names none is the same for every part. Nothing has to cross between parts.
All inputs are finite; a program needn't handle non-finite values.
Results may differ from a plain program's by a relative error of at most 0.00011.
Values sent between devices are 32-bit elements; how exact they have to be, the bound alone decides.
A program may use at most 128 MiB of HBM per device.

v0:
```python
import functools
import math

import jax
import jax.numpy as jnp
import numpy as np
from jax import lax
from jax.experimental import pallas as pl
from jax.experimental.pallas import tpu as pltpu
from jax.sharding import PartitionSpec as P

kerr_scale = 0.1
MESH = pl.DeviceIdType.MESH
f32 = jnp.float32
bf16 = jnp.bfloat16


def split_table(table):
    high = table.astype(np.float32).astype(bf16)
    low = (table - high.astype(np.float64)).astype(np.float32).astype(bf16)
    return np.stack([np.asarray(high), np.asarray(low)])


def real_form(size):
    turns = np.outer(np.arange(size), np.arange(size)) % size
    angle = turns * (2.0 * math.pi / size)
    cosine, sine = np.cos(angle), np.sin(angle)
    return np.block([[cosine, sine], [-sine, cosine]])


def make_tables(outer, total):
    left, right = real_form(outer), real_form(128)
    turns = np.outer(np.arange(outer), np.arange(128)) % total
    angle = turns * (2.0 * math.pi / total)
    twist = np.stack([np.cos(angle), -np.sin(angle)]).astype(np.float32)
    return (
        split_table(left),
        split_table(left.T / total),
        split_table(right.T),
        split_table(right),
        twist,
    )


def halves(value):
    high = value.astype(bf16)
    return high, (value - high.astype(f32)).astype(bf16)


def mm(a, b):
    return jnp.dot(a, b, preferred_element_type=f32)


def left_dot(table, value):
    high, low = halves(value)
    return mm(table[0], high) + (mm(table[0], low) + mm(table[1], high))


def right_dot(value, table):
    high, low = halves(value)
    return mm(high, table[0]) + (mm(low, table[0]) + mm(high, table[1]))


def farthest_first(me, count):
    low, high = jnp.int32(0), jnp.int32(count - 1)
    peers = []
    for _ in range(count - 1):
        up = (high - me >= me - low).astype(jnp.int32)
        peers.append(up * high + (1 - up) * low)
        high, low = high - up, low + 1 - up
    return peers


def kernel(
    sizes, kind, pairs, x, target, margin, beta_hbm,
    left_f_hbm, left_i_hbm, right_f_hbm, right_i_hbm, twist_hbm, out,
    left_f, left_i, right_f, right_i, twist, beta, phase_tab,
    rows_in, send_z, kb, t1, t2, mg, mg_s, prods, coup, grad_pair, moved, cots, grads, rows_back, send_out,
    table_sem, own_sem, in_s, in_r, mg_ss, mg_r, t1_s, t1_r, t2_s, t2_r, kb_s, kb_r, gb_s, gb_r, out_s, out_r,
):
    Dt, Dm, B, Bl, ml, M, A, Al, As, Ak, J, total = sizes
    me_t = lax.axis_index("tm")
    me_m = lax.axis_index("mode")
    tm_peers = farthest_first(me_t, Dt)
    mode_peers = farthest_first(me_m, Dm)

    def remote(src, dst, send, recv, axis, peer):
        return pltpu.make_async_remote_copy(
            src_ref=src, dst_ref=dst, send_sem=send, recv_sem=recv, device_id={axis: peer}, device_id_type=MESH
        )

    barrier = pltpu.get_barrier_semaphore()
    for peer in tm_peers:
        pl.semaphore_signal(barrier, inc=1, device_id={"tm": peer}, device_id_type=MESH)
    for peer in mode_peers:
        pl.semaphore_signal(barrier, inc=1, device_id={"mode": peer}, device_id_type=MESH)
    pl.semaphore_wait(barrier, Dt + Dm - 2)

    sends = []
    owns = {}
    own_count = [0]

    def go(src, dst, send, recv, axis, peer):
        copy = remote(src, dst, send, recv, axis, peer)
        copy.start()
        sends.append(copy)

    def own(name, src, dst):
        copy = pltpu.make_async_copy(src, dst, own_sem.at[own_count[0]])
        own_count[0] += 1
        copy.start()
        owns[name] = copy

    def target_part(i, b):
        if (As * ml) % 8 == 0:
            return target.at[:, :, b, pl.ds(pl.multiple_of(i * (As * ml), 8), As * ml), :]
        return target.at[i, :, :, b]

    def target_first_leg(b):
        for peer in mode_peers:
            go(target_part(peer, b), t1[b].at[me_m], t1_s.at[b, peer], t1_r.at[b, me_m], "mode", peer)
        own(("t1", b), target_part(me_m, b), t1[b].at[me_m])

    def target_second_leg(b):
        owns[("t1", b)].wait()
        for peer in mode_peers:
            remote(target_part(0, b), t1[b].at[peer], t1_s.at[b, peer], t1_r.at[b, peer], "mode", peer).wait_recv()
        for peer in tm_peers:
            go(t1[b].at[:, :, peer], t2[b].at[me_t], t2_s.at[b, peer], t2_r.at[b, me_t], "tm", peer)
        own(("t2", b), t1[b].at[:, :, me_t], t2[b].at[me_t])

    for b in range(Bl):
        for peer in tm_peers:
            go(x.at[:, peer * Bl + b], rows_in.at[b, me_t], in_s.at[b, peer], in_r.at[b, me_t], "tm", peer)
        own(("in", b), x.at[:, me_t * Bl + b], rows_in.at[b, me_t])
    for peer in mode_peers:
        go(margin, mg.at[me_m], mg_ss.at[peer], mg_r.at[me_m], "mode", peer)
    own("mg", margin, mg.at[me_m])
    target_first_leg(0)
    table_copies = []
    for spot, (src, dst) in enumerate(
        ((left_f_hbm, left_f), (left_i_hbm, left_i), (right_f_hbm, right_f), (right_i_hbm, right_i), (twist_hbm, twist), (beta_hbm, beta))
    ):
        copy = pltpu.make_async_copy(src, dst, table_sem.at[spot])
        copy.start()
        table_copies.append(copy)

    for copy in table_copies:
        copy.wait()
    low_digit = lax.broadcasted_iota(jnp.int32, (A, 128), 0)
    high_digit = lax.broadcasted_iota(jnp.int32, (A, 128), 1)
    frequency = low_digit + A * high_digit
    signed = jnp.where(frequency < total // 2, frequency, frequency - total).astype(f32)
    omega = signed * (8.0 / total)
    for m in range(ml):
        phase = (
            beta[0, m, kind[0]] * omega
            + beta[1, m, kind[0]] * (omega * omega) / 2.0
            + beta[2, m, kind[0]] * (omega * omega * omega) / 6.0
        )
        phase_tab[0, m * A : (m + 1) * A, :] = jnp.cos(phase)
        phase_tab[1, m * A : (m + 1) * A, :] = jnp.sin(phase)
    def disperse(stacked, direction):
        spun = left_dot(left_f, stacked)
        tw_r, tw_i = twist[0], twist[1]
        blocks = []
        for m in range(ml):
            re = spun[:A, m * 128 : (m + 1) * 128]
            im = spun[A:, m * 128 : (m + 1) * 128]
            blocks.append(jnp.concatenate([re * tw_r - im * tw_i, re * tw_i + im * tw_r], axis=1))
        spectrum = right_dot(jnp.concatenate(blocks, axis=0), right_f)
        re, im = spectrum[:, :128], spectrum[:, 128:]
        cosine = phase_tab[0]
        sine = phase_tab[1] * direction
        turned = jnp.concatenate([re * cosine - im * sine, re * sine + im * cosine], axis=1)
        back = right_dot(turned, right_i)
        real_rows, imag_rows = [], []
        for m in range(ml):
            re = back[m * A : (m + 1) * A, :128]
            im = back[m * A : (m + 1) * A, 128:]
            real_rows.append(re * tw_r + im * tw_i)
            imag_rows.append(im * tw_r - re * tw_i)
        joined = jnp.concatenate(
            [jnp.concatenate(real_rows, axis=1), jnp.concatenate(imag_rows, axis=1)], axis=0
        )
        return left_dot(left_i, joined)

    for b in range(Bl):
        owns[("in", b)].wait()
        for peer in tm_peers:
            remote(x.at[:, b], rows_in.at[b, peer], in_s.at[b, peer], in_r.at[b, peer], "tm", peer).wait_recv()
        stacked = jnp.concatenate(
            [
                jnp.concatenate(
                    [rows_in[b, j, ri, pl.ds(m, Al, stride=ml), :] for ri in range(2) for j in range(Dt)], axis=0
                )
                for m in range(ml)
            ],
            axis=1,
        )
        result = disperse(stacked, 1.0)
        for i in range(Dm):
            for m in range(ml):
                for ri in range(2):
                    for j in range(Dt):
                        row = ri * A + j * Al + i * As
                        send_z[i, b, m, ri, j * As : (j + 1) * As, :] = result[row : row + As, m * 128 : (m + 1) * 128]
        for peer in mode_peers:
            go(send_z.at[peer, b], kb[b].at[pl.ds(me_m * ml, ml)], kb_s.at[b, peer], kb_r.at[b, me_m], "mode", peer)
        own(("kb", b), send_z.at[me_m, b], kb[b].at[pl.ds(me_m * ml, ml)])
        if b + 1 < Bl:
            target_first_leg(b + 1)
        if b == 0:
            target_second_leg(0)

    owns["mg"].wait()
    for peer in mode_peers:
        remote(margin, mg.at[peer], mg_ss.at[peer], mg_r.at[peer], "mode", peer).wait_recv()
    own("mgs", mg, mg_s)
    owns["mgs"].wait()

    zero = jnp.zeros((Ak, 128), f32)

    def weight(p, n, j):
        return mg_s[p // ml, lax.rem(p, ml), n * J + j]

    for b in range(Bl):
        owns[("kb", b)].wait()
        for peer in mode_peers:
            remote(
                send_z.at[0, b], kb[b].at[pl.ds(peer * ml, ml)], kb_s.at[b, peer], kb_r.at[b, peer], "mode", peer
            ).wait_recv()
        owns[("t2", b)].wait()
        for peer in tm_peers:
            remote(t1[b].at[:, :, 0], t2[b].at[peer], t2_s.at[b, peer], t2_r.at[b, peer], "tm", peer).wait_recv()

        @pl.loop(0, J)
        def _(j):
            first, second = pairs[0, j], pairs[1, j]
            ar, ai = kb[b][first, 0], kb[b][first, 1]
            br, bi = kb[b][second, 0], kb[b][second, 1]
            prods[j, 0] = ar * br - ai * bi
            prods[j, 1] = ar * bi + ai * br

        @pl.loop(0, M)
        def _(p):
            def inner(step, carry):
                kr, ki = carry
                sums = [zero] * 4
                for j in range(J):
                    pr, pi = prods[j, 0], prods[j, 1]
                    for s in range(2):
                        w = weight(p, step * 2 + s, j)
                        sums[2 * s] = sums[2 * s] + w * pr
                        sums[2 * s + 1] = sums[2 * s + 1] + w * pi
                for s in range(2):
                    n = step * 2 + s
                    cr, ci = sums[2 * s], sums[2 * s + 1]
                    coup[p * M + n, 0] = cr
                    coup[p * M + n, 1] = ci
                    ur, ui = kb[b][n, 0], kb[b][n, 1]
                    kr = kr + (cr * ur + ci * ui)
                    ki = ki + (ci * ur - cr * ui)
                return kr, ki

            kr, ki = lax.fori_loop(0, M // 2, inner, (zero, zero), unroll=4)
            owner, local = p // ml, lax.rem(p, ml)
            wanted = [
                jnp.concatenate(
                    [t2[b][j, owner, ri, pl.ds(local, As, stride=ml), :] for j in range(Dt)], axis=0
                )
                for ri in range(2)
            ]
            cots[p, 0] = 2.0 * (kb[b][p, 0] - kerr_scale * ki - wanted[0])
            cots[p, 1] = 2.0 * (kb[b][p, 1] + kerr_scale * kr - wanted[1])

        @pl.loop(0, M)
        def _(n):
            ur, ui = kb[b][n, 0], kb[b][n, 1]

            def inner(p, carry):
                gr, gi = carry
                er, ei = kerr_scale * cots[p, 1], -kerr_scale * cots[p, 0]
                cr, ci = coup[p * M + n, 0], coup[p * M + n, 1]
                gr = gr + (er * cr + ei * ci)
                gi = gi + (er * ci - ei * cr)
                coup[p * M + n, 0] = er * ur - ei * ui
                coup[p * M + n, 1] = er * ui + ei * ur
                return gr, gi

            gr, gi = lax.fori_loop(0, M, inner, (cots[n, 0], cots[n, 1]), unroll=8)
            grads[b, n, 0] = gr
            grads[b, n, 1] = gi

        @pl.loop(0, J // 4)
        def _(quad):
            def outer(p, carry):
                sums = list(carry)
                for n in range(M):
                    sr, si = coup[p * M + n, 0], coup[p * M + n, 1]
                    for s in range(4):
                        w = weight(p, n, quad * 4 + s)
                        sums[2 * s] = sums[2 * s] + w * sr
                        sums[2 * s + 1] = sums[2 * s + 1] + w * si
                return tuple(sums)

            sums = lax.fori_loop(0, M, outer, (zero,) * 8)
            for s in range(4):
                grad_pair[quad * 4 + s, 0] = sums[2 * s]
                grad_pair[quad * 4 + s, 1] = sums[2 * s + 1]

        @pl.loop(0, J)
        def _(j):
            gr, gi = grad_pair[j, 0], grad_pair[j, 1]
            for side, other in ((0, 1), (1, 0)):
                vr, vi = kb[b][pairs[other, j], 0], kb[b][pairs[other, j], 1]
                moved[side, j, 0] = vr * gr + vi * gi
                moved[side, j, 1] = vr * gi - vi * gr

        @pl.loop(0, M)
        def _(n):
            gr, gi = grads[b, n, 0], grads[b, n, 1]
            for j in range(J):
                for side in range(2):
                    w = (pairs[side, j] == n).astype(f32)
                    gr = gr + w * moved[side, j, 0]
                    gi = gi + w * moved[side, j, 1]
            grads[b, n, 0] = gr
            grads[b, n, 1] = gi

        for peer in mode_peers:
            go(grads.at[b, pl.ds(peer * ml, ml)], rows_back.at[b, me_m], gb_s.at[b, peer], gb_r.at[b, me_m], "mode", peer)
        if b + 1 < Bl:
            target_second_leg(b + 1)
        own(("gb", b), grads.at[b, pl.ds(me_m * ml, ml)], rows_back.at[b, me_m])

    for b in range(Bl):
        owns[("gb", b)].wait()
        for peer in mode_peers:
            remote(
                grads.at[b, pl.ds(0, ml)], rows_back.at[b, peer], gb_s.at[b, peer], gb_r.at[b, peer], "mode", peer
            ).wait_recv()
        stacked = jnp.concatenate(
            [
                jnp.concatenate(
                    [
                        rows_back[b, i, m, ri, j * As : (j + 1) * As, :]
                        for ri in range(2)
                        for j in range(Dt)
                        for i in range(Dm)
                    ],
                    axis=0,
                )
                for m in range(ml)
            ],
            axis=1,
        )
        result = disperse(stacked, -1.0)
        for j in range(Dt):
            for ri in range(2):
                for m in range(ml):
                    row = ri * A + j * Al
                    send_out[j, b, ri, pl.ds(m, Al, stride=ml), :] = result[row : row + Al, m * 128 : (m + 1) * 128]
        for peer in tm_peers:
            go(send_out.at[peer, b], out.at[:, me_t * Bl + b], out_s.at[b, peer], out_r.at[b, me_t], "tm", peer)
        own(("out", b), send_out.at[me_t, b], out.at[:, me_t * Bl + b])
    for b in range(Bl):
        owns[("out", b)].wait()
        for peer in tm_peers:
            remote(
                send_out.at[0, b], out.at[:, peer * Bl + b], out_s.at[b, peer], out_r.at[b, peer], "tm", peer
            ).wait_recv()
    for copy in sends:
        copy.wait_send()


def on_device(Dm, Dt, input_field, target_field, margin, pair_index, mode_beta, segment_kind):
    _, B, ml, Tl = input_field.shape
    M, J = margin.shape[1], margin.shape[2]
    total = Tl * Dt
    A = total // 128
    Al = Tl // 128
    Bl = B // Dt
    As = Al // Dm
    Ak = As * Dt
    def by_rows(values):
        return values.reshape(2, B, ml, Al, 128).transpose(0, 1, 3, 2, 4).reshape(2, B, Al * ml, 128)

    x = by_rows(input_field)
    target = by_rows(target_field).reshape(2, Dt, Bl, Al * ml, 128)
    if (As * ml) % 8:
        target = target.reshape(2, Dt, Bl, Dm, As * ml, 128).transpose(3, 0, 1, 2, 4, 5)
    tables = make_tables(A, total)
    sizes = (Dt, Dm, B, Bl, ml, M, A, Al, As, Ak, J, total)
    vm = lambda *shape: pltpu.VMEM(shape, f32)
    dma = lambda *shape: pltpu.SemaphoreType.DMA(shape)
    anyspace = pl.BlockSpec(memory_space=pl.ANY)
    smem = pl.BlockSpec(memory_space=pltpu.SMEM)
    vmem = pl.BlockSpec(memory_space=pltpu.VMEM)
    out = pl.pallas_call(
        functools.partial(kernel, sizes),
        out_shape=jax.ShapeDtypeStruct((2, B, Al * ml, 128), f32),
        in_specs=[smem] * 2 + [anyspace, anyspace, vmem] + [anyspace] * 6,
        out_specs=vmem,
        scratch_shapes=[pltpu.VMEM(t.shape, bf16) for t in tables[:4]]
        + [
            vm(2, A, 128),
            pltpu.SMEM((3, ml, mode_beta.shape[0]), f32),
            vm(2, ml * A, 128),
            vm(Bl, Dt, 2, Al * ml, 128),
            vm(Dm, Bl, ml, 2, Ak, 128),
            [vm(M, 2, Ak, 128) for _ in range(Bl)],
            [vm(Dm, 2, Dt, As * ml, 128) for _ in range(Bl)],
            [vm(Dt, Dm, 2, As * ml, 128) for _ in range(Bl)],
            vm(Dm, ml, M * J),
            pltpu.SMEM((Dm, ml, M * J), f32),
            vm(J, 2, Ak, 128),
            vm(M * M, 2, Ak, 128),
            vm(J, 2, Ak, 128),
            vm(2, J, 2, Ak, 128),
            vm(M, 2, Ak, 128),
            vm(Bl, M, 2, Ak, 128),
            vm(Bl, Dm, ml, 2, Ak, 128),
            vm(Dt, Bl, 2, Al * ml, 128),
            dma(6),
            dma(6 * Bl + 2),
            dma(Bl, Dt), dma(Bl, Dt),
            dma(Dm), dma(Dm),
            dma(Bl, Dm), dma(Bl, Dm),
            dma(Bl, Dt), dma(Bl, Dt),
            dma(Bl, Dm), dma(Bl, Dm),
            dma(Bl, Dm), dma(Bl, Dm),
            dma(Bl, Dt), dma(Bl, Dt),
        ],
        compiler_params=pltpu.CompilerParams(collective_id=0, has_side_effects=True, vmem_limit_bytes=62 * 1024 * 1024),
    )(segment_kind, pair_index.T, x, target, margin.reshape(ml, M * J), mode_beta.transpose(2, 1, 0), *[jnp.asarray(t) for t in tables])
    return out.reshape(2, B, Al, ml, 128).transpose(0, 1, 3, 2, 4).reshape(2, B, ml, Tl)


def solution(mesh):
    return jax.shard_map(
        functools.partial(on_device, mesh.shape["mode"], mesh.shape["tm"]),
        mesh=mesh,
        in_specs=(
            P(None, "dp", "mode", "tm"),
            P(None, "dp", "mode", "tm"),
            P("mode", None, None),
            P(),
            P(None, "mode", None),
            P(),
        ),
        out_specs=P(None, "dp", "mode", "tm"),
        check_vma=False,
    )
```

profile of v0, /device:TPU:0, one launch (start us, length us, event | category | flops | bytes accessed | tf_op | source)
XLA Modules:
  0.0 57.2 jit_solution(15180059203204597182)
XLA Ops:
  0.0 0.0 copy-start
  0.7 0.0 copy-done
  0.7 0.6 %reshape.21.margin = f32[2,128]{1,0:T(2,128)} reshape(f32[2,8,16]{2,1,0:T(8,128)S(1)} %copy-done) | data formatting | bytes 2048 | tf_op jit(solution)/shard_map/reshape | solution.py:436
  1.3 54.0 %shard_map.109 = f32[2,8,64,128]{3,2,1,0:T(8,128)} custom-call(s32[1]{0:T(128)S(6)} %copy.16.kind, s32[2,16]{1,0:T(2,128)} %bitcast.21, f32[2,8,64,128]{3,2,1,0:T(8,128)} %bitcast.18, f32[2,4,2,64,128]{4,3,2,1,0:T(8,128)} %bitcast.19, f32[2,128]{1,0:T(2,128)} %reshape.21.margin, f32[3,2,1024]{2,1,0:T(2,128)} %bitcast.20, ...), custom_call_target="tpu_custom_call" | custom-call | tf_op jit(solution)/shard_map/pallas_call | solution.py:400
  55.3 1.9 %copy.17 = f32[2,8,2,4096]{3,2,1,0:T(2,128)} copy(f32[2,8,2,4096]{3,2,1,0:T(2,128)} %bitcast.17) | data formatting | bytes 1048576
Async XLA Ops:
  0.0 0.7 %copy-start = (f32[2,8,16]{2,1,0:T(8,128)S(1)}, f32[2,8,16]{2,1,0:T(8,128)}, u32[]{:S(2)}) copy-start(f32[2,8,16]{2,1,0:T(8,128)} %param.13) | copy-start | bytes 3076
where the time goes:
time: 57.4 us; the launch traced here: 57.2 us
  Pallas kernels  54 us (94%)
  local copies, waits for them, and re-layouts  2.56 us (4%)
  between operations  0.68 us (1%)
    pallas_call x1, Pallas kernels, on_device(): pl.pallas_call(functools.partial(kernel, sizes), out_shape=jax.ShapeDtype...  54 us
    unnamed x3, local copies, waits for them, and re-layouts  1.92 us

commit v1 on v0

--- a/solution.py
+++ b/solution.py
@@ -71,11 +71,84 @@
     return peers
 
 
+def digits(shape, axis):
+    return lax.broadcasted_iota(jnp.int32, shape, axis)
+
+
+def one_hot(condition):
+    return jnp.where(condition, 1.0, 0.0).astype(bf16)
+
+
+def make_weights(sizes, pairs, mg, w1, w2, spread):
+    Dt, Dm, B, Bl, ml, M, A, Al, As, Ak, J, total = sizes
+    depth = J * 8
+    group = max(1, 64 // M)
+    step = group * M
+
+    rows, cols = digits((step * 8, step), 0), digits((step * 8, step), 1)
+    taller = one_hot(rows // 8 == cols)
+    rows, cols = digits((2 * J, 3 * depth), 0), digits((2 * J, 3 * depth), 1)
+    wider = one_hot((rows == cols % depth // 8 + jnp.where(cols < 2 * depth, 0, J)))
+    kept = digits((step * 8, 3 * depth), 0) % 8 == digits((step * 8, 3 * depth), 1) % 8
+
+    def block(p):
+        return mg[p // ml, p % ml]
+
+    columns = []
+    for g in range(M // group):
+        values = jnp.concatenate([block(g * group + i) for i in range(group)], axis=0)
+        high, low = halves(values)
+        both = jnp.concatenate([high.astype(f32), low.astype(f32)], axis=1).astype(bf16)
+        tall = mm(taller, both).astype(bf16)
+        wide = mm(tall, wider)
+        w1[g * step * 8 : (g + 1) * step * 8, :] = jnp.where(kept, wide, 0.0).astype(bf16)
+        columns.append((high, low))
+
+    rows, cols = digits((depth, J), 0), digits((depth, J), 1)
+    lifter = one_hot(rows // 8 == cols)
+
+    def turned(values):
+        return lax.dot_general(lifter, values, (((1,), (1,)), ((), ())), preferred_element_type=f32).astype(bf16)
+
+    lifted = [[turned(part) for part in pair] for pair in columns]
+    width = M * 8
+    kept = digits((depth, 3 * width), 0) % 8 == digits((depth, 3 * width), 1) % 8
+    rows, cols = digits((step, 3 * width), 0), digits((step, 3 * width), 1)
+
+    def fill(n):
+        total = jnp.zeros((depth, 3 * width), f32)
+        for g, parts in enumerate(lifted):
+            for which, part in enumerate(parts):
+                inside = (cols >= 2 * width) if which else (cols < 2 * width)
+                match = (rows // M + g * group == cols % width // 8) & (rows % M == n) & inside
+                total = total + mm(part, one_hot(match))
+        w2[pl.ds(pl.multiple_of(n * depth, depth), depth), :] = jnp.where(kept, total, 0.0).astype(bf16)
+
+    if M <= 8:
+        for n in range(M):
+            fill(n)
+    else:
+        pl.loop(0, M)(fill)
+
+    which = digits((8, 2 * depth), 1) // 8
+    chosen = jnp.zeros((8, 2 * depth), jnp.int32)
+    for side in range(2):
+        for j in range(J):
+            chosen = jnp.where(which == side * J + j, pairs[side, j], chosen)
+    shape = (width, 2 * depth)
+    match = (digits(shape, 0) // 8 == jnp.concatenate([chosen] * M, axis=0)) & (
+        digits(shape, 0) % 8 == digits(shape, 1) % 8
+    )
+    spread[:, : 2 * depth] = one_hot(match)
+    spread[:, 2 * depth :] = one_hot(match)
+
+
 def kernel(
     sizes, kind, pairs, x, target, margin, beta_hbm,
     left_f_hbm, left_i_hbm, right_f_hbm, right_i_hbm, twist_hbm, out,
     left_f, left_i, right_f, right_i, twist, beta, phase_tab,
-    rows_in, send_z, kb, t1, t2, mg, mg_s, prods, coup, grad_pair, moved, cots, grads, rows_back, send_out,
+    rows_in, send_z, kb, t1, t2, mg, w1, w2, spread, pair_cols, coup, wanted, cots, push, push_cols, turn, move_cols,
+    grads, rows_back, send_out,
     table_sem, own_sem, in_s, in_r, mg_ss, mg_r, t1_s, t1_r, t2_s, t2_r, kb_s, kb_r, gb_s, gb_r, out_s, out_r,
 ):
     Dt, Dm, B, Bl, ml, M, A, Al, As, Ak, J, total = sizes
@@ -185,6 +258,126 @@
         )
         return left_dot(left_i, joined)
 
+    owns["mg"].wait()
+    for peer in mode_peers:
+        remote(margin, mg.at[peer], mg_ss.at[peer], mg_r.at[peer], "mode", peer).wait_recv()
+    make_weights(sizes, pairs, mg, w1, w2, spread)
+
+    def kerr(b):
+        field = kb[b]
+        tiles = Ak // 8
+        depth = J * 8
+
+        for j in range(0, J, 2):
+            made = []
+            for s in range(2):
+                first, second = pairs[0, j + s], pairs[1, j + s]
+                ar, ai = field[first, 0], field[first, 1]
+                br, bi = field[second, 0], field[second, 1]
+                made.append((ar * br - ai * bi, ar * bi + ai * br))
+            for q in range(tiles):
+                for ri in range(2):
+                    high, low = halves(
+                        jnp.concatenate([made[s][ri][q * 8 : q * 8 + 8] for s in range(2)], axis=0)
+                    )
+                    cols = pl.ds((2 * q + ri) * 128, 128)
+                    pair_cols[j * 8 : j * 8 + 16, cols] = high
+                    pair_cols[depth + j * 8 : depth + j * 8 + 16, cols] = low
+                    pair_cols[2 * depth + j * 8 : 2 * depth + j * 8 + 16, cols] = high
+        for q in range(tiles):
+            cols = pl.ds(q * 256, 256)
+            coup[:, cols] = mm(w1[...], pair_cols[:, cols])
+
+        @pl.loop(0, M)
+        def _(p):
+            owner, local = p // ml, lax.rem(p, ml)
+            for ri in range(2):
+                wanted[p, ri] = jnp.concatenate(
+                    [t2[b][j, owner, ri, pl.ds(local, As, stride=ml), :] for j in range(Dt)], axis=0
+                )
+
+        @pl.loop(0, M // 2)
+        def _(pp):
+            for q in range(tiles):
+                rows = pl.ds(q * 8, 8)
+                pushed = []
+                for s in range(2):
+                    p = pp * 2 + s
+                    kr = ki = jnp.zeros((8, 128), f32)
+                    for n in range(M):
+                        at = pl.ds(pl.multiple_of((p * M + n) * 8, 8), 8)
+                        cr, ci = coup[at, q * 256 : q * 256 + 128], coup[at, q * 256 + 128 : q * 256 + 256]
+                        ur, ui = field[n, 0, rows], field[n, 1, rows]
+                        kr = kr + (cr * ur + ci * ui)
+                        ki = ki + (ci * ur - cr * ui)
+                    cr = 2.0 * (field[p, 0, rows] - kerr_scale * ki - wanted[p, 0, rows])
+                    ci = 2.0 * (field[p, 1, rows] + kerr_scale * kr - wanted[p, 1, rows])
+                    cots[p, 0, rows] = cr
+                    cots[p, 1, rows] = ci
+                    pushed.append((kerr_scale * ci, -kerr_scale * cr))
+                    push[p, 0, rows] = pushed[s][0]
+                    push[p, 1, rows] = pushed[s][1]
+                for ri in range(2):
+                    high, low = halves(jnp.concatenate([pushed[s][ri] for s in range(2)], axis=0))
+                    cols = pl.ds((2 * q + ri) * 128, 128)
+                    for part, value in enumerate((high, low, high)):
+                        push_cols[pl.ds(pl.multiple_of(part * (M * 8) + pp * 16, 16), 16), cols] = value
+
+        for q in range(tiles):
+            cols = pl.ds(q * 256, 256)
+            turn[:, cols] = mm(w2[...], push_cols[:, cols])
+
+        @pl.loop(0, M)
+        def _(n):
+            for q in range(tiles):
+                rows = pl.ds(q * 8, 8)
+                gr, gi = cots[n, 0, rows], cots[n, 1, rows]
+                for p in range(M):
+                    at = pl.ds(pl.multiple_of((p * M + n) * 8, 8), 8)
+                    cr, ci = coup[at, q * 256 : q * 256 + 128], coup[at, q * 256 + 128 : q * 256 + 256]
+                    er, ei = push[p, 0, rows], push[p, 1, rows]
+                    gr = gr + (er * cr + ei * ci)
+                    gi = gi + (er * ci - ei * cr)
+                cots[n, 0, rows] = gr
+                cots[n, 1, rows] = gi
+
+        @pl.loop(0, J // 2)
+        def _(jj):
+            for q in range(tiles):
+                rows = pl.ds(q * 8, 8)
+                moved = []
+                for s in range(2):
+                    j = jj * 2 + s
+                    gr = gi = jnp.zeros((8, 128), f32)
+                    for n in range(M):
+                        at = pl.ds(pl.multiple_of((n * J + j) * 8, 8), 8)
+                        tr, ti = turn[at, q * 256 : q * 256 + 128], turn[at, q * 256 + 128 : q * 256 + 256]
+                        ur, ui = field[n, 0, rows], field[n, 1, rows]
+                        gr = gr + (tr * ur - ti * ui)
+                        gi = gi + (tr * ui + ti * ur)
+                    for side in range(2):
+                        other = pairs[1 - side, j]
+                        vr, vi = field[other, 0, rows], field[other, 1, rows]
+                        moved.append((side, (vr * gr + vi * gi, vr * gi - vi * gr)))
+                for side in range(2):
+                    for ri in range(2):
+                        high, low = halves(
+                            jnp.concatenate([value[ri] for which, value in moved if which == side], axis=0)
+                        )
+                        cols = pl.ds((2 * q + ri) * 128, 128)
+                        at = side * depth + jj * 16
+                        move_cols[pl.ds(pl.multiple_of(at, 16), 16), cols] = high
+                        move_cols[pl.ds(pl.multiple_of(2 * depth + at, 16), 16), cols] = low
+
+        for q in range(tiles):
+            rows = pl.ds(q * 8, 8)
+            back = mm(spread[...], move_cols[:, q * 256 : q * 256 + 256])
+            for n in range(M):
+                for ri in range(2):
+                    grads[b, n, ri, rows] = (
+                        cots[n, ri, rows] + back[n * 8 : n * 8 + 8, ri * 128 : ri * 128 + 128]
+                    )
+
     for b in range(Bl):
         owns[("in", b)].wait()
         for peer in tm_peers:
@@ -213,17 +406,6 @@
         if b == 0:
             target_second_leg(0)
 
-    owns["mg"].wait()
-    for peer in mode_peers:
-        remote(margin, mg.at[peer], mg_ss.at[peer], mg_r.at[peer], "mode", peer).wait_recv()
-    own("mgs", mg, mg_s)
-    owns["mgs"].wait()
-
-    zero = jnp.zeros((Ak, 128), f32)
-
-    def weight(p, n, j):
-        return mg_s[p // ml, lax.rem(p, ml), n * J + j]
-
     for b in range(Bl):
         owns[("kb", b)].wait()
         for peer in mode_peers:
@@ -234,99 +416,7 @@
         for peer in tm_peers:
             remote(t1[b].at[:, :, 0], t2[b].at[peer], t2_s.at[b, peer], t2_r.at[b, peer], "tm", peer).wait_recv()
 
-        @pl.loop(0, J)
-        def _(j):
-            first, second = pairs[0, j], pairs[1, j]
-            ar, ai = kb[b][first, 0], kb[b][first, 1]
-            br, bi = kb[b][second, 0], kb[b][second, 1]
-            prods[j, 0] = ar * br - ai * bi
-            prods[j, 1] = ar * bi + ai * br
-
-        @pl.loop(0, M)
-        def _(p):
-            def inner(step, carry):
-                kr, ki = carry
-                sums = [zero] * 4
-                for j in range(J):
-                    pr, pi = prods[j, 0], prods[j, 1]
-                    for s in range(2):
-                        w = weight(p, step * 2 + s, j)
-                        sums[2 * s] = sums[2 * s] + w * pr
-                        sums[2 * s + 1] = sums[2 * s + 1] + w * pi
-                for s in range(2):
-                    n = step * 2 + s
-                    cr, ci = sums[2 * s], sums[2 * s + 1]
-                    coup[p * M + n, 0] = cr
-                    coup[p * M + n, 1] = ci
-                    ur, ui = kb[b][n, 0], kb[b][n, 1]
-                    kr = kr + (cr * ur + ci * ui)
-                    ki = ki + (ci * ur - cr * ui)
-                return kr, ki
-
-            kr, ki = lax.fori_loop(0, M // 2, inner, (zero, zero), unroll=4)
-            owner, local = p // ml, lax.rem(p, ml)
-            wanted = [
-                jnp.concatenate(
-                    [t2[b][j, owner, ri, pl.ds(local, As, stride=ml), :] for j in range(Dt)], axis=0
-                )
-                for ri in range(2)
-            ]
-            cots[p, 0] = 2.0 * (kb[b][p, 0] - kerr_scale * ki - wanted[0])
-            cots[p, 1] = 2.0 * (kb[b][p, 1] + kerr_scale * kr - wanted[1])
-
-        @pl.loop(0, M)
-        def _(n):
-            ur, ui = kb[b][n, 0], kb[b][n, 1]
-
-            def inner(p, carry):
-                gr, gi = carry
-                er, ei = kerr_scale * cots[p, 1], -kerr_scale * cots[p, 0]
-                cr, ci = coup[p * M + n, 0], coup[p * M + n, 1]
-                gr = gr + (er * cr + ei * ci)
-                gi = gi + (er * ci - ei * cr)
-                coup[p * M + n, 0] = er * ur - ei * ui
-                coup[p * M + n, 1] = er * ui + ei * ur
-                return gr, gi
-
-            gr, gi = lax.fori_loop(0, M, inner, (cots[n, 0], cots[n, 1]), unroll=8)
-            grads[b, n, 0] = gr
-            grads[b, n, 1] = gi
-
-        @pl.loop(0, J // 4)
-        def _(quad):
-            def outer(p, carry):
-                sums = list(carry)
-                for n in range(M):
-                    sr, si = coup[p * M + n, 0], coup[p * M + n, 1]
-                    for s in range(4):
-                        w = weight(p, n, quad * 4 + s)
-                        sums[2 * s] = sums[2 * s] + w * sr
-                        sums[2 * s + 1] = sums[2 * s + 1] + w * si
-                return tuple(sums)
-
-            sums = lax.fori_loop(0, M, outer, (zero,) * 8)
-            for s in range(4):
-                grad_pair[quad * 4 + s, 0] = sums[2 * s]
-                grad_pair[quad * 4 + s, 1] = sums[2 * s + 1]
-
-        @pl.loop(0, J)
-        def _(j):
-            gr, gi = grad_pair[j, 0], grad_pair[j, 1]
-            for side, other in ((0, 1), (1, 0)):
-                vr, vi = kb[b][pairs[other, j], 0], kb[b][pairs[other, j], 1]
-                moved[side, j, 0] = vr * gr + vi * gi
-                moved[side, j, 1] = vr * gi - vi * gr
-
-        @pl.loop(0, M)
-        def _(n):
-            gr, gi = grads[b, n, 0], grads[b, n, 1]
-            for j in range(J):
-                for side in range(2):
-                    w = (pairs[side, j] == n).astype(f32)
-                    gr = gr + w * moved[side, j, 0]
-                    gi = gi + w * moved[side, j, 1]
-            grads[b, n, 0] = gr
-            grads[b, n, 1] = gi
+        kerr(b)
 
         for peer in mode_peers:
             go(grads.at[b, pl.ds(peer * ml, ml)], rows_back.at[b, me_m], gb_s.at[b, peer], gb_r.at[b, me_m], "mode", peer)
@@ -393,6 +483,7 @@
     tables = make_tables(A, total)
     sizes = (Dt, Dm, B, Bl, ml, M, A, Al, As, Ak, J, total)
     vm = lambda *shape: pltpu.VMEM(shape, f32)
+    vb = lambda *shape: pltpu.VMEM(shape, bf16)
     dma = lambda *shape: pltpu.SemaphoreType.DMA(shape)
     anyspace = pl.BlockSpec(memory_space=pl.ANY)
     smem = pl.BlockSpec(memory_space=pltpu.SMEM)
@@ -412,13 +503,18 @@
             [vm(M, 2, Ak, 128) for _ in range(Bl)],
             [vm(Dm, 2, Dt, As * ml, 128) for _ in range(Bl)],
             [vm(Dt, Dm, 2, As * ml, 128) for _ in range(Bl)],
-            vm(Dm, ml, M * J),
-            pltpu.SMEM((Dm, ml, M * J), f32),
-            vm(J, 2, Ak, 128),
-            vm(M * M, 2, Ak, 128),
-            vm(J, 2, Ak, 128),
-            vm(2, J, 2, Ak, 128),
+            vm(Dm, ml, M, J),
+            vb(M * M * 8, 3 * J * 8),
+            vb(M * J * 8, 3 * M * 8),
+            vb(M * 8, 4 * J * 8),
+            vb(3 * J * 8, Ak * 32),
+            vm(M * M * 8, Ak * 32),
             vm(M, 2, Ak, 128),
+            vm(M, 2, Ak, 128),
+            vm(M, 2, Ak, 128),
+            vb(3 * M * 8, Ak * 32),
+            vm(M * J * 8, Ak * 32),
+            vb(4 * J * 8, Ak * 32),
             vm(Bl, M, 2, Ak, 128),
             vm(Bl, Dm, ml, 2, Ak, 128),
             vm(Dt, Bl, 2, Al * ml, 128),
@@ -433,7 +529,7 @@
             dma(Bl, Dt), dma(Bl, Dt),
         ],
         compiler_params=pltpu.CompilerParams(collective_id=0, has_side_effects=True, vmem_limit_bytes=62 * 1024 * 1024),
-    )(segment_kind, pair_index.T, x, target, margin.reshape(ml, M * J), mode_beta.transpose(2, 1, 0), *[jnp.asarray(t) for t in tables])
+    )(segment_kind, pair_index.T, x, target, margin, mode_beta.transpose(2, 1, 0), *[jnp.asarray(t) for t in tables])
     return out.reshape(2, B, Al, ml, 128).transpose(0, 1, 3, 2, 4).reshape(2, B, ml, Tl)
 
 

time: 57.4 us -> 53 us (0.923)
  Pallas kernels: 54 us -> 50.2 us
  local copies, waits for them, and re-layouts: 2.56 us -> 1.89 us
    pallas_call x1, Pallas kernels: 54 us -> 50.2 us  [on_device(): pl.pallas_call(functools.partial(kernel, sizes), out_shape=jax.ShapeDtype...]
    reshape x1 -> x0, local copies, waits for them, and re-layouts: 0.64 us -> none  [on_device(): margin.reshape(ml, M * J)]
    unnamed x3 -> x1, local copies, waits for them, and re-layouts: 1.92 us -> 1.89 us
where the time goes in v1:
time: 53 us; the launch traced here: 52.8 us
  Pallas kernels  50.2 us (95%)
  local copies, waits for them, and re-layouts  1.89 us (4%)
  between operations  0.66 us (1%)
    pallas_call x1, Pallas kernels, on_device(): pl.pallas_call(functools.partial(kernel, sizes), out_shape=jax.ShapeDtype...  50.2 us
    unnamed x1, local copies, waits for them, and re-layouts  1.89 us

profile of v1, /device:TPU:0, one launch (start us, length us, event | category | flops | bytes accessed | tf_op | source)
XLA Modules:
  0.0 52.8 jit_solution(11808361784429016209)
XLA Ops:
  0.7 50.2 %shard_map.109 = f32[2,8,64,128]{3,2,1,0:T(8,128)} custom-call(s32[1]{0:T(128)S(6)} %copy.16.kind, s32[2,16]{1,0:T(2,128)} %bitcast.21, f32[2,8,64,128]{3,2,1,0:T(8,128)} %bitcast.18, f32[2,4,2,64,128]{4,3,2,1,0:T(8,128)} %bitcast.19, f32[2,8,16]{2,1,0:T(8,128)} %margin.1, f32[3,2,1024]{2,1,0:T(2,128)} %bitcast.20, ...), custom_call_target="tpu_custom_call" | custom-call | tf_op jit(solution)/shard_map/pallas_call | solution.py:491
  50.9 1.9 %copy.17 = f32[2,8,2,4096]{3,2,1,0:T(2,128)} copy(f32[2,8,2,4096]{3,2,1,0:T(2,128)} %bitcast.17) | data formatting | bytes 1048576

commit v2 on v1

--- a/solution.py
+++ b/solution.py
@@ -146,10 +146,10 @@
 def kernel(
     sizes, kind, pairs, x, target, margin, beta_hbm,
     left_f_hbm, left_i_hbm, right_f_hbm, right_i_hbm, twist_hbm, out,
-    left_f, left_i, right_f, right_i, twist, beta, phase_tab,
+    x_near, target_near, left_f, left_i, right_f, right_i, twist, beta, phase_tab,
     rows_in, send_z, kb, t1, t2, mg, w1, w2, spread, pair_cols, coup, wanted, cots, push, push_cols, turn, move_cols,
     grads, rows_back, send_out,
-    table_sem, own_sem, in_s, in_r, mg_ss, mg_r, t1_s, t1_r, t2_s, t2_r, kb_s, kb_r, gb_s, gb_r, out_s, out_r,
+    near_sem, table_sem, own_sem, in_s, in_r, mg_ss, mg_r, t1_s, t1_r, t2_s, t2_r, kb_s, kb_r, gb_s, gb_r, out_s, out_r,
 ):
     Dt, Dm, B, Bl, ml, M, A, Al, As, Ak, J, total = sizes
     me_t = lax.axis_index("tm")
@@ -162,6 +162,10 @@
             src_ref=src, dst_ref=dst, send_sem=send, recv_sem=recv, device_id={axis: peer}, device_id_type=MESH
         )
 
+    staged = [pltpu.make_async_copy(x, x_near, near_sem.at[0]), pltpu.make_async_copy(target, target_near, near_sem.at[1])]
+    for copy in staged:
+        copy.start()
+
     barrier = pltpu.get_barrier_semaphore()
     for peer in tm_peers:
         pl.semaphore_signal(barrier, inc=1, device_id={"tm": peer}, device_id_type=MESH)
@@ -186,8 +190,8 @@
 
     def target_part(i, b):
         if (As * ml) % 8 == 0:
-            return target.at[:, :, b, pl.ds(pl.multiple_of(i * (As * ml), 8), As * ml), :]
-        return target.at[i, :, :, b]
+            return target_near.at[:, :, b, pl.ds(pl.multiple_of(i * (As * ml), 8), As * ml), :]
+        return target_near.at[i, :, :, b]
 
     def target_first_leg(b):
         for peer in mode_peers:
@@ -202,14 +206,17 @@
             go(t1[b].at[:, :, peer], t2[b].at[me_t], t2_s.at[b, peer], t2_r.at[b, me_t], "tm", peer)
         own(("t2", b), t1[b].at[:, :, me_t], t2[b].at[me_t])
 
+    staged[0].wait()
     for b in range(Bl):
         for peer in tm_peers:
-            go(x.at[:, peer * Bl + b], rows_in.at[b, me_t], in_s.at[b, peer], in_r.at[b, me_t], "tm", peer)
-        own(("in", b), x.at[:, me_t * Bl + b], rows_in.at[b, me_t])
+            go(x_near.at[:, peer * Bl + b], rows_in.at[b, me_t], in_s.at[b, peer], in_r.at[b, me_t], "tm", peer)
+        own(("in", b), x_near.at[:, me_t * Bl + b], rows_in.at[b, me_t])
     for peer in mode_peers:
         go(margin, mg.at[me_m], mg_ss.at[peer], mg_r.at[me_m], "mode", peer)
     own("mg", margin, mg.at[me_m])
-    target_first_leg(0)
+    staged[1].wait()
+    for b in range(Bl):
+        target_first_leg(b)
     table_copies = []
     for spot, (src, dst) in enumerate(
         ((left_f_hbm, left_f), (left_i_hbm, left_i), (right_f_hbm, right_f), (right_i_hbm, right_i), (twist_hbm, twist), (beta_hbm, beta))
@@ -233,22 +240,24 @@
         )
         phase_tab[0, m * A : (m + 1) * A, :] = jnp.cos(phase)
         phase_tab[1, m * A : (m + 1) * A, :] = jnp.sin(phase)
-    def disperse(stacked, direction):
+    def disperse(stacked, direction, modes):
         spun = left_dot(left_f, stacked)
         tw_r, tw_i = twist[0], twist[1]
         blocks = []
-        for m in range(ml):
+        for m in range(len(modes)):
             re = spun[:A, m * 128 : (m + 1) * 128]
             im = spun[A:, m * 128 : (m + 1) * 128]
             blocks.append(jnp.concatenate([re * tw_r - im * tw_i, re * tw_i + im * tw_r], axis=1))
         spectrum = right_dot(jnp.concatenate(blocks, axis=0), right_f)
         re, im = spectrum[:, :128], spectrum[:, 128:]
-        cosine = phase_tab[0]
-        sine = phase_tab[1] * direction
+        cosine, sine = (
+            jnp.concatenate([phase_tab[part, m * A : (m + 1) * A, :] for m in modes], axis=0) for part in range(2)
+        )
+        sine = sine * direction
         turned = jnp.concatenate([re * cosine - im * sine, re * sine + im * cosine], axis=1)
         back = right_dot(turned, right_i)
         real_rows, imag_rows = [], []
-        for m in range(ml):
+        for m in range(len(modes)):
             re = back[m * A : (m + 1) * A, :128]
             im = back[m * A : (m + 1) * A, 128:]
             real_rows.append(re * tw_r + im * tw_i)
@@ -257,11 +266,6 @@
             [jnp.concatenate(real_rows, axis=1), jnp.concatenate(imag_rows, axis=1)], axis=0
         )
         return left_dot(left_i, joined)
-
-    owns["mg"].wait()
-    for peer in mode_peers:
-        remote(margin, mg.at[peer], mg_ss.at[peer], mg_r.at[peer], "mode", peer).wait_recv()
-    make_weights(sizes, pairs, mg, w1, w2, spread)
 
     def kerr(b):
         field = kb[b]
@@ -381,7 +385,7 @@
     for b in range(Bl):
         owns[("in", b)].wait()
         for peer in tm_peers:
-            remote(x.at[:, b], rows_in.at[b, peer], in_s.at[b, peer], in_r.at[b, peer], "tm", peer).wait_recv()
+            remote(x_near.at[:, b], rows_in.at[b, peer], in_s.at[b, peer], in_r.at[b, peer], "tm", peer).wait_recv()
         stacked = jnp.concatenate(
             [
                 jnp.concatenate(
@@ -391,7 +395,7 @@
             ],
             axis=1,
         )
-        result = disperse(stacked, 1.0)
+        result = disperse(stacked, 1.0, range(ml))
         for i in range(Dm):
             for m in range(ml):
                 for ri in range(2):
@@ -401,10 +405,15 @@
         for peer in mode_peers:
             go(send_z.at[peer, b], kb[b].at[pl.ds(me_m * ml, ml)], kb_s.at[b, peer], kb_r.at[b, me_m], "mode", peer)
         own(("kb", b), send_z.at[me_m, b], kb[b].at[pl.ds(me_m * ml, ml)])
-        if b + 1 < Bl:
-            target_first_leg(b + 1)
         if b == 0:
             target_second_leg(0)
+
+    owns["mg"].wait()
+    for peer in mode_peers:
+        remote(margin, mg.at[peer], mg_ss.at[peer], mg_r.at[peer], "mode", peer).wait_recv()
+    make_weights(sizes, pairs, mg, w1, w2, spread)
+    for b in range(1, Bl):
+        target_second_leg(b)
 
     for b in range(Bl):
         owns[("kb", b)].wait()
@@ -418,50 +427,65 @@
 
         kerr(b)
 
-        for peer in mode_peers:
-            go(grads.at[b, pl.ds(peer * ml, ml)], rows_back.at[b, me_m], gb_s.at[b, peer], gb_r.at[b, me_m], "mode", peer)
-        if b + 1 < Bl:
-            target_second_leg(b + 1)
-        own(("gb", b), grads.at[b, pl.ds(me_m * ml, ml)], rows_back.at[b, me_m])
+        for m in range(ml):
+            for peer in mode_peers:
+                go(
+                    grads.at[b, peer * ml + m], rows_back.at[b, m, me_m],
+                    gb_s.at[b, m, peer], gb_r.at[b, m, me_m], "mode", peer,
+                )
+            own(("gb", b, m), grads.at[b, me_m * ml + m], rows_back.at[b, m, me_m])
 
     for b in range(Bl):
-        owns[("gb", b)].wait()
-        for peer in mode_peers:
-            remote(
-                grads.at[b, pl.ds(0, ml)], rows_back.at[b, peer], gb_s.at[b, peer], gb_r.at[b, peer], "mode", peer
-            ).wait_recv()
-        stacked = jnp.concatenate(
-            [
-                jnp.concatenate(
-                    [
-                        rows_back[b, i, m, ri, j * As : (j + 1) * As, :]
-                        for ri in range(2)
-                        for j in range(Dt)
-                        for i in range(Dm)
-                    ],
-                    axis=0,
+        for m in range(ml):
+            owns[("gb", b, m)].wait()
+            for peer in mode_peers:
+                remote(
+                    grads.at[b, m], rows_back.at[b, m, peer], gb_s.at[b, m, peer], gb_r.at[b, m, peer], "mode", peer
+                ).wait_recv()
+            stacked = jnp.concatenate(
+                [
+                    rows_back[b, m, i, ri, j * As : (j + 1) * As, :]
+                    for ri in range(2)
+                    for j in range(Dt)
+                    for i in range(Dm)
+                ],
+                axis=0,
+            )
+            result = disperse(stacked, -1.0, [m])
+            for j in range(Dt):
+                for ri in range(2):
+                    row = ri * A + j * Al
+                    send_out[j, b, m, ri] = result[row : row + Al, :]
+            for peer in tm_peers:
+                go(
+                    send_out.at[peer, b, m], out.at[:, me_t * Bl + b, m],
+                    out_s.at[b, m, peer], out_r.at[b, m, me_t], "tm", peer,
                 )
-                for m in range(ml)
-            ],
-            axis=1,
-        )
-        result = disperse(stacked, -1.0)
-        for j in range(Dt):
-            for ri in range(2):
-                for m in range(ml):
-                    row = ri * A + j * Al
-                    send_out[j, b, ri, pl.ds(m, Al, stride=ml), :] = result[row : row + Al, m * 128 : (m + 1) * 128]
-        for peer in tm_peers:
-            go(send_out.at[peer, b], out.at[:, me_t * Bl + b], out_s.at[b, peer], out_r.at[b, me_t], "tm", peer)
-        own(("out", b), send_out.at[me_t, b], out.at[:, me_t * Bl + b])
+            own(("out", b, m), send_out.at[me_t, b, m], out.at[:, me_t * Bl + b, m])
     for b in range(Bl):
-        owns[("out", b)].wait()
-        for peer in tm_peers:
-            remote(
-                send_out.at[0, b], out.at[:, peer * Bl + b], out_s.at[b, peer], out_r.at[b, peer], "tm", peer
-            ).wait_recv()
+        for m in range(ml):
+            owns[("out", b, m)].wait()
+            for peer in tm_peers:
+                remote(
+                    send_out.at[0, b, m], out.at[:, peer * Bl + b, m],
+                    out_s.at[b, m, peer], out_r.at[b, m, peer], "tm", peer,
+                ).wait_recv()
     for copy in sends:
         copy.wait_send()
+
+
+def finish(gathered, out, woven, sem):
+    _, B, ml, Al, _ = gathered.shape
+    copies = []
+    for b in range(B):
+        for ri in range(2):
+            for m in range(ml):
+                woven[ri, b, pl.ds(m, Al, stride=ml), :] = gathered[ri, b, m]
+        copy = pltpu.make_async_copy(woven.at[:, b], out.at[:, b], sem.at[b])
+        copy.start()
+        copies.append(copy)
+    for copy in copies:
+        copy.wait()
 
 
 def on_device(Dm, Dt, input_field, target_field, margin, pair_index, mode_beta, segment_kind):
@@ -488,12 +512,13 @@
     anyspace = pl.BlockSpec(memory_space=pl.ANY)
     smem = pl.BlockSpec(memory_space=pltpu.SMEM)
     vmem = pl.BlockSpec(memory_space=pltpu.VMEM)
-    out = pl.pallas_call(
+    gathered = pl.pallas_call(
         functools.partial(kernel, sizes),
-        out_shape=jax.ShapeDtypeStruct((2, B, Al * ml, 128), f32),
+        out_shape=pltpu.VMEM((2, B, ml, Al, 128), f32),
         in_specs=[smem] * 2 + [anyspace, anyspace, vmem] + [anyspace] * 6,
         out_specs=vmem,
-        scratch_shapes=[pltpu.VMEM(t.shape, bf16) for t in tables[:4]]
+        scratch_shapes=[vm(*x.shape), vm(*target.shape)]
+        + [pltpu.VMEM(t.shape, bf16) for t in tables[:4]]
         + [
             vm(2, A, 128),
             pltpu.SMEM((3, ml, mode_beta.shape[0]), f32),
@@ -516,20 +541,28 @@
             vm(M * J * 8, Ak * 32),
             vb(4 * J * 8, Ak * 32),
             vm(Bl, M, 2, Ak, 128),
-            vm(Bl, Dm, ml, 2, Ak, 128),
-            vm(Dt, Bl, 2, Al * ml, 128),
+            vm(Bl, ml, Dm, 2, Ak, 128),
+            vm(Dt, Bl, ml, 2, Al, 128),
+            dma(2),
             dma(6),
-            dma(6 * Bl + 2),
+            dma((4 + 2 * ml) * Bl + 1),
             dma(Bl, Dt), dma(Bl, Dt),
             dma(Dm), dma(Dm),
             dma(Bl, Dm), dma(Bl, Dm),
             dma(Bl, Dt), dma(Bl, Dt),
             dma(Bl, Dm), dma(Bl, Dm),
-            dma(Bl, Dm), dma(Bl, Dm),
-            dma(Bl, Dt), dma(Bl, Dt),
+            dma(Bl, ml, Dm), dma(Bl, ml, Dm),
+            dma(Bl, ml, Dt), dma(Bl, ml, Dt),
         ],
         compiler_params=pltpu.CompilerParams(collective_id=0, has_side_effects=True, vmem_limit_bytes=62 * 1024 * 1024),
     )(segment_kind, pair_index.T, x, target, margin, mode_beta.transpose(2, 1, 0), *[jnp.asarray(t) for t in tables])
+    out = pl.pallas_call(
+        finish,
+        out_shape=jax.ShapeDtypeStruct((2, B, Al * ml, 128), f32),
+        in_specs=[vmem],
+        out_specs=anyspace,
+        scratch_shapes=[vm(2, B, Al * ml, 128), dma(B)],
+    )(pltpu.with_memory_space_constraint(gathered, pltpu.VMEM))
     return out.reshape(2, B, Al, ml, 128).transpose(0, 1, 3, 2, 4).reshape(2, B, ml, Tl)
 
 

time: 53 us -> 50.3 us (0.949)
  local copies, waits for them, and re-layouts: 1.89 us -> 0 us
  Pallas kernels: 50.2 us -> 49.4 us
    unnamed x1 -> x0, local copies, waits for them, and re-layouts: 1.89 us -> none
    pallas_call x1 -> x2, Pallas kernels: 50.2 us -> 49.4 us  [the longest x1 48.6 us: on_device(): pl.pallas_call(functools.partial(kernel, sizes), out_shape=pltpu.VMEM((2,...]
where the time goes in v2:
time: 50.3 us; the launch traced here: 50.1 us
  Pallas kernels  49.4 us (98%)
  between operations  0.66 us (1%)
    pallas_call x1, Pallas kernels, on_device(): pl.pallas_call(functools.partial(kernel, sizes), out_shape=pltpu.VMEM((2,...  48.6 us

profile of v2, /device:TPU:0, one launch (start us, length us, event | category | flops | bytes accessed | tf_op | source)
XLA Modules:
  0.0 50.1 jit_solution(80804635033150727)
XLA Ops:
  0.7 48.6 %shard_map.109.gathered = f32[2,8,2,32,128]{4,3,2,1,0:T(8,128)S(1)} custom-call(s32[1]{0:T(128)S(6)} %copy.15.kind, s32[2,16]{1,0:T(2,128)} %bitcast.20, f32[2,8,64,128]{3,2,1,0:T(8,128)} %bitcast.17, f32[2,4,2,64,128]{4,3,2,1,0:T(8,128)} %bitcast.18, f32[2,8,16]{2,1,0:T(8,128)} %margin.1, f32[3,2,1024]{2,1,0:T(2,128)} %bitcast.19, ...), custom_call_target="tpu_custom_call" | custom-call | tf_op jit(solution)/shard_map/pallas_call | solution.py:515
  49.2 0.9 %shard_map.110 = f32[2,8,64,128]{3,2,1,0:T(8,128)} custom-call(f32[2,8,2,32,128]{4,3,2,1,0:T(8,128)S(1)} %shard_map.109.gathered), custom_call_target="tpu_custom_call" | custom-call | tf_op jit(solution)/shard_map/pallas_call | solution.py:559

commit v3 on v2

--- a/solution.py
+++ b/solution.py
@@ -144,14 +144,16 @@
 
 
 def kernel(
-    sizes, kind, pairs, x, target, margin, beta_hbm,
+    sizes, kind_hbm, pairs_hbm, x, target, margin_hbm, beta_hbm,
     left_f_hbm, left_i_hbm, right_f_hbm, right_i_hbm, twist_hbm, out,
-    x_near, target_near, left_f, left_i, right_f, right_i, twist, beta, phase_tab,
+    x_near, target_near, kind, pairs, margin, left_f, left_i, right_f, right_i, twist, beta, phase_tab,
     rows_in, send_z, kb, t1, t2, mg, w1, w2, spread, pair_cols, coup, wanted, cots, push, push_cols, turn, move_cols,
     grads, rows_back, send_out,
     near_sem, table_sem, own_sem, in_s, in_r, mg_ss, mg_r, t1_s, t1_r, t2_s, t2_r, kb_s, kb_r, gb_s, gb_r, out_s, out_r,
 ):
     Dt, Dm, B, Bl, ml, M, A, Al, As, Ak, J, total = sizes
+    parts = 2 if Ak % 16 == 0 else 1
+    Hk = Ak // parts
     me_t = lax.axis_index("tm")
     me_m = lax.axis_index("mode")
     tm_peers = farthest_first(me_t, Dt)
@@ -162,15 +164,17 @@
             src_ref=src, dst_ref=dst, send_sem=send, recv_sem=recv, device_id={axis: peer}, device_id_type=MESH
         )
 
-    staged = [pltpu.make_async_copy(x, x_near, near_sem.at[0]), pltpu.make_async_copy(target, target_near, near_sem.at[1])]
-    for copy in staged:
-        copy.start()
-
     barrier = pltpu.get_barrier_semaphore()
+    for peer in mode_peers:
+        pl.semaphore_signal(barrier, inc=1, device_id={"mode": peer}, device_id_type=MESH)
     for peer in tm_peers:
         pl.semaphore_signal(barrier, inc=1, device_id={"tm": peer}, device_id_type=MESH)
-    for peer in mode_peers:
-        pl.semaphore_signal(barrier, inc=1, device_id={"mode": peer}, device_id_type=MESH)
+    staged = []
+    for spot, (src, dst) in enumerate(
+        ((margin_hbm, margin), (target, target_near), (x, x_near), (kind_hbm, kind), (pairs_hbm, pairs))
+    ):
+        staged.append(pltpu.make_async_copy(src, dst, near_sem.at[spot]))
+        staged[-1].start()
     pl.semaphore_wait(barrier, Dt + Dm - 2)
 
     sends = []
@@ -207,16 +211,20 @@
         own(("t2", b), t1[b].at[:, :, me_t], t2[b].at[me_t])
 
     staged[0].wait()
+    for peer in mode_peers:
+        go(margin, mg.at[me_m], mg_ss.at[peer], mg_r.at[me_m], "mode", peer)
+    own("mg", margin, mg.at[me_m])
+    staged[1].wait()
+    target_first_leg(0)
+    staged[2].wait()
     for b in range(Bl):
         for peer in tm_peers:
             go(x_near.at[:, peer * Bl + b], rows_in.at[b, me_t], in_s.at[b, peer], in_r.at[b, me_t], "tm", peer)
         own(("in", b), x_near.at[:, me_t * Bl + b], rows_in.at[b, me_t])
-    for peer in mode_peers:
-        go(margin, mg.at[me_m], mg_ss.at[peer], mg_r.at[me_m], "mode", peer)
-    own("mg", margin, mg.at[me_m])
-    staged[1].wait()
-    for b in range(Bl):
+    for b in range(1, Bl):
         target_first_leg(b)
+    for copy in staged[3:]:
+        copy.wait()
     table_copies = []
     for spot, (src, dst) in enumerate(
         ((left_f_hbm, left_f), (left_i_hbm, left_i), (right_f_hbm, right_f), (right_i_hbm, right_i), (twist_hbm, twist), (beta_hbm, beta))
@@ -267,9 +275,25 @@
         )
         return left_dot(left_i, joined)
 
-    def kerr(b):
-        field = kb[b]
-        tiles = Ak // 8
+    def send_gradient(b, h, m, peer):
+        rows = pl.ds(h * Hk, Hk)
+        go(
+            grads.at[b, peer * ml + m, :, rows], rows_back.at[b, m, me_m, :, rows],
+            gb_s.at[b, h, m, peer], gb_r.at[b, h, m, me_m], "mode", peer,
+        )
+
+    def line_up(b):
+        @pl.loop(0, M)
+        def _(p):
+            owner, local = p // ml, lax.rem(p, ml)
+            for ri in range(2):
+                wanted[p, ri] = jnp.concatenate(
+                    [t2[b][j, owner, ri, pl.ds(local, As, stride=ml), :] for j in range(Dt)], axis=0
+                )
+
+    def kerr(b, h):
+        field = kb[b * parts + h]
+        tiles = Hk // 8
         depth = J * 8
 
         for j in range(0, J, 2):
@@ -292,18 +316,10 @@
             cols = pl.ds(q * 256, 256)
             coup[:, cols] = mm(w1[...], pair_cols[:, cols])
 
-        @pl.loop(0, M)
-        def _(p):
-            owner, local = p // ml, lax.rem(p, ml)
-            for ri in range(2):
-                wanted[p, ri] = jnp.concatenate(
-                    [t2[b][j, owner, ri, pl.ds(local, As, stride=ml), :] for j in range(Dt)], axis=0
-                )
-
         @pl.loop(0, M // 2)
         def _(pp):
             for q in range(tiles):
-                rows = pl.ds(q * 8, 8)
+                rows, here = pl.ds(h * Hk + q * 8, 8), pl.ds(q * 8, 8)
                 pushed = []
                 for s in range(2):
                     p = pp * 2 + s
@@ -311,11 +327,11 @@
                     for n in range(M):
                         at = pl.ds(pl.multiple_of((p * M + n) * 8, 8), 8)
                         cr, ci = coup[at, q * 256 : q * 256 + 128], coup[at, q * 256 + 128 : q * 256 + 256]
-                        ur, ui = field[n, 0, rows], field[n, 1, rows]
+                        ur, ui = field[n, 0, here], field[n, 1, here]
                         kr = kr + (cr * ur + ci * ui)
                         ki = ki + (ci * ur - cr * ui)
-                    cr = 2.0 * (field[p, 0, rows] - kerr_scale * ki - wanted[p, 0, rows])
-                    ci = 2.0 * (field[p, 1, rows] + kerr_scale * kr - wanted[p, 1, rows])
+                    cr = 2.0 * (field[p, 0, here] - kerr_scale * ki - wanted[p, 0, rows])
+                    ci = 2.0 * (field[p, 1, here] + kerr_scale * kr - wanted[p, 1, rows])
                     cots[p, 0, rows] = cr
                     cots[p, 1, rows] = ci
                     pushed.append((kerr_scale * ci, -kerr_scale * cr))
@@ -334,7 +350,7 @@
         @pl.loop(0, M)
         def _(n):
             for q in range(tiles):
-                rows = pl.ds(q * 8, 8)
+                rows, here = pl.ds(h * Hk + q * 8, 8), pl.ds(q * 8, 8)
                 gr, gi = cots[n, 0, rows], cots[n, 1, rows]
                 for p in range(M):
                     at = pl.ds(pl.multiple_of((p * M + n) * 8, 8), 8)
@@ -348,7 +364,7 @@
         @pl.loop(0, J // 2)
         def _(jj):
             for q in range(tiles):
-                rows = pl.ds(q * 8, 8)
+                rows, here = pl.ds(h * Hk + q * 8, 8), pl.ds(q * 8, 8)
                 moved = []
                 for s in range(2):
                     j = jj * 2 + s
@@ -356,12 +372,12 @@
                     for n in range(M):
                         at = pl.ds(pl.multiple_of((n * J + j) * 8, 8), 8)
                         tr, ti = turn[at, q * 256 : q * 256 + 128], turn[at, q * 256 + 128 : q * 256 + 256]
-                        ur, ui = field[n, 0, rows], field[n, 1, rows]
+                        ur, ui = field[n, 0, here], field[n, 1, here]
                         gr = gr + (tr * ur - ti * ui)
                         gi = gi + (tr * ui + ti * ur)
                     for side in range(2):
                         other = pairs[1 - side, j]
-                        vr, vi = field[other, 0, rows], field[other, 1, rows]
+                        vr, vi = field[other, 0, here], field[other, 1, here]
                         moved.append((side, (vr * gr + vi * gi, vr * gi - vi * gr)))
                 for side in range(2):
                     for ri in range(2):
@@ -374,7 +390,7 @@
                         move_cols[pl.ds(pl.multiple_of(2 * depth + at, 16), 16), cols] = low
 
         for q in range(tiles):
-            rows = pl.ds(q * 8, 8)
+            rows = pl.ds(h * Hk + q * 8, 8)
             back = mm(spread[...], move_cols[:, q * 256 : q * 256 + 256])
             for n in range(M):
                 for ri in range(2):
@@ -401,10 +417,15 @@
                 for ri in range(2):
                     for j in range(Dt):
                         row = ri * A + j * Al + i * As
-                        send_z[i, b, m, ri, j * As : (j + 1) * As, :] = result[row : row + As, m * 128 : (m + 1) * 128]
-        for peer in mode_peers:
-            go(send_z.at[peer, b], kb[b].at[pl.ds(me_m * ml, ml)], kb_s.at[b, peer], kb_r.at[b, me_m], "mode", peer)
-        own(("kb", b), send_z.at[me_m, b], kb[b].at[pl.ds(me_m * ml, ml)])
+                        h, at = j * As // Hk, j * As % Hk
+                        send_z[i, b, h, m, ri, at : at + As, :] = result[row : row + As, m * 128 : (m + 1) * 128]
+        for h in range(parts):
+            for peer in mode_peers:
+                go(
+                    send_z.at[peer, b, h], kb[b * parts + h].at[pl.ds(me_m * ml, ml)],
+                    kb_s.at[b, h, peer], kb_r.at[b, h, me_m], "mode", peer,
+                )
+            own(("kb", b, h), send_z.at[me_m, b, h], kb[b * parts + h].at[pl.ds(me_m * ml, ml)])
         if b == 0:
             target_second_leg(0)
 
@@ -416,32 +437,40 @@
         target_second_leg(b)
 
     for b in range(Bl):
-        owns[("kb", b)].wait()
-        for peer in mode_peers:
-            remote(
-                send_z.at[0, b], kb[b].at[pl.ds(peer * ml, ml)], kb_s.at[b, peer], kb_r.at[b, peer], "mode", peer
-            ).wait_recv()
         owns[("t2", b)].wait()
         for peer in tm_peers:
             remote(t1[b].at[:, :, 0], t2[b].at[peer], t2_s.at[b, peer], t2_r.at[b, peer], "tm", peer).wait_recv()
-
-        kerr(b)
-
+        line_up(b)
+        for h in range(parts):
+            owns[("kb", b, h)].wait()
+            for peer in mode_peers:
+                remote(
+                    send_z.at[0, b, h], kb[b * parts + h].at[pl.ds(peer * ml, ml)],
+                    kb_s.at[b, h, peer], kb_r.at[b, h, peer], "mode", peer,
+                ).wait_recv()
+            kerr(b, h)
+            if b + 1 < Bl:
+                for m in range(ml):
+                    for peer in mode_peers:
+                        send_gradient(b, h, m, peer)
+        if b + 1 == Bl:
+            for peer in mode_peers:
+                for m in range(ml):
+                    for h in range(parts):
+                        send_gradient(b, h, m, peer)
         for m in range(ml):
-            for peer in mode_peers:
-                go(
-                    grads.at[b, peer * ml + m], rows_back.at[b, m, me_m],
-                    gb_s.at[b, m, peer], gb_r.at[b, m, me_m], "mode", peer,
-                )
             own(("gb", b, m), grads.at[b, me_m * ml + m], rows_back.at[b, m, me_m])
 
     for b in range(Bl):
         for m in range(ml):
             owns[("gb", b, m)].wait()
             for peer in mode_peers:
-                remote(
-                    grads.at[b, m], rows_back.at[b, m, peer], gb_s.at[b, m, peer], gb_r.at[b, m, peer], "mode", peer
-                ).wait_recv()
+                for h in range(parts):
+                    rows = pl.ds(h * Hk, Hk)
+                    remote(
+                        grads.at[b, m, :, rows], rows_back.at[b, m, peer, :, rows],
+                        gb_s.at[b, h, m, peer], gb_r.at[b, h, m, peer], "mode", peer,
+                    ).wait_recv()
             stacked = jnp.concatenate(
                 [
                     rows_back[b, m, i, ri, j * As : (j + 1) * As, :]
@@ -497,6 +526,8 @@
     Bl = B // Dt
     As = Al // Dm
     Ak = As * Dt
+    parts = 2 if Ak % 16 == 0 else 1
+    Hk = Ak // parts
     def by_rows(values):
         return values.reshape(2, B, ml, Al, 128).transpose(0, 1, 3, 2, 4).reshape(2, B, Al * ml, 128)
 
@@ -510,48 +541,53 @@
     vb = lambda *shape: pltpu.VMEM(shape, bf16)
     dma = lambda *shape: pltpu.SemaphoreType.DMA(shape)
     anyspace = pl.BlockSpec(memory_space=pl.ANY)
-    smem = pl.BlockSpec(memory_space=pltpu.SMEM)
     vmem = pl.BlockSpec(memory_space=pltpu.VMEM)
     gathered = pl.pallas_call(
         functools.partial(kernel, sizes),
         out_shape=pltpu.VMEM((2, B, ml, Al, 128), f32),
-        in_specs=[smem] * 2 + [anyspace, anyspace, vmem] + [anyspace] * 6,
+        in_specs=[anyspace] * 11,
         out_specs=vmem,
-        scratch_shapes=[vm(*x.shape), vm(*target.shape)]
+        scratch_shapes=[
+            vm(*x.shape),
+            vm(*target.shape),
+            pltpu.SMEM(segment_kind.shape, jnp.int32),
+            pltpu.SMEM(pair_index.shape[::-1], jnp.int32),
+            vm(ml, M, J),
+        ]
         + [pltpu.VMEM(t.shape, bf16) for t in tables[:4]]
         + [
             vm(2, A, 128),
             pltpu.SMEM((3, ml, mode_beta.shape[0]), f32),
             vm(2, ml * A, 128),
             vm(Bl, Dt, 2, Al * ml, 128),
-            vm(Dm, Bl, ml, 2, Ak, 128),
-            [vm(M, 2, Ak, 128) for _ in range(Bl)],
+            vm(Dm, Bl, parts, ml, 2, Hk, 128),
+            [vm(M, 2, Hk, 128) for _ in range(Bl * parts)],
             [vm(Dm, 2, Dt, As * ml, 128) for _ in range(Bl)],
             [vm(Dt, Dm, 2, As * ml, 128) for _ in range(Bl)],
             vm(Dm, ml, M, J),
             vb(M * M * 8, 3 * J * 8),
             vb(M * J * 8, 3 * M * 8),
             vb(M * 8, 4 * J * 8),
-            vb(3 * J * 8, Ak * 32),
-            vm(M * M * 8, Ak * 32),
+            vb(3 * J * 8, Hk * 32),
+            vm(M * M * 8, Hk * 32),
             vm(M, 2, Ak, 128),
             vm(M, 2, Ak, 128),
             vm(M, 2, Ak, 128),
-            vb(3 * M * 8, Ak * 32),
-            vm(M * J * 8, Ak * 32),
-            vb(4 * J * 8, Ak * 32),
+            vb(3 * M * 8, Hk * 32),
+            vm(M * J * 8, Hk * 32),
+            vb(4 * J * 8, Hk * 32),
             vm(Bl, M, 2, Ak, 128),
             vm(Bl, ml, Dm, 2, Ak, 128),
             vm(Dt, Bl, ml, 2, Al, 128),
-            dma(2),
+            dma(5),
             dma(6),
-            dma((4 + 2 * ml) * Bl + 1),
+            dma((3 + parts + 2 * ml) * Bl + 1),
             dma(Bl, Dt), dma(Bl, Dt),
             dma(Dm), dma(Dm),
             dma(Bl, Dm), dma(Bl, Dm),
             dma(Bl, Dt), dma(Bl, Dt),
-            dma(Bl, Dm), dma(Bl, Dm),
-            dma(Bl, ml, Dm), dma(Bl, ml, Dm),
+            dma(Bl, parts, Dm), dma(Bl, parts, Dm),
+            dma(Bl, parts, ml, Dm), dma(Bl, parts, ml, Dm),
             dma(Bl, ml, Dt), dma(Bl, ml, Dt),
         ],
         compiler_params=pltpu.CompilerParams(collective_id=0, has_side_effects=True, vmem_limit_bytes=62 * 1024 * 1024),

time: 50.3 us -> 48.6 us (0.966)
  Pallas kernels: 49.4 us -> 47.8 us
    pallas_call x1, Pallas kernels: 48.6 us -> 46.9 us  [on_device(): pl.pallas_call(functools.partial(kernel, sizes), out_shape=pltpu.VMEM((2,...]
where the time goes in v3:
time: 48.6 us; the launch traced here: 48.5 us
  Pallas kernels  47.8 us (98%)
  between operations  0.66 us (1%)
    pallas_call x1, Pallas kernels, on_device(): pl.pallas_call(functools.partial(kernel, sizes), out_shape=pltpu.VMEM((2,...  46.9 us

profile of v3, /device:TPU:0, one launch (start us, length us, event | category | flops | bytes accessed | tf_op | source)
XLA Modules:
  0.0 48.5 jit_solution(17629350443845976615)
XLA Ops:
  0.7 46.9 %shard_map.109.gathered = f32[2,8,2,32,128]{4,3,2,1,0:T(8,128)S(1)} custom-call(s32[1]{0:T(128)S(6)} %copy.15.kind_hbm, s32[2,16]{1,0:T(2,128)} %bitcast.20, f32[2,8,64,128]{3,2,1,0:T(8,128)} %bitcast.17, f32[2,4,2,64,128]{4,3,2,1,0:T(8,128)} %bitcast.18, f32[2,8,16]{2,1,0:T(8,128)} %margin_hbm.1, f32[3,2,1024]{2,1,0:T(2,128)} %bitcast.19, ...), custom_call_target="tpu_custom_call" | custom-call | tf_op jit(solution)/shard_map/pallas_call | solution.py:545
  47.6 0.9 %shard_map.110 = f32[2,8,64,128]{3,2,1,0:T(8,128)} custom-call(f32[2,8,2,32,128]{4,3,2,1,0:T(8,128)S(1)} %shard_map.109.gathered), custom_call_target="tpu_custom_call" | custom-call | tf_op jit(solution)/shard_map/pallas_call | solution.py:595

commit v4 on v3

--- a/solution.py
+++ b/solution.py
@@ -147,9 +147,9 @@
     sizes, kind_hbm, pairs_hbm, x, target, margin_hbm, beta_hbm,
     left_f_hbm, left_i_hbm, right_f_hbm, right_i_hbm, twist_hbm, out,
     x_near, target_near, kind, pairs, margin, left_f, left_i, right_f, right_i, twist, beta, phase_tab,
-    rows_in, send_z, kb, t1, t2, mg, w1, w2, spread, pair_cols, coup, wanted, cots, push, push_cols, turn, move_cols,
+    rows_in, send_z, kb, t1, t2, mg, w1, w2, spread, pair_cols, coup, wanted, cots, push, push_cols, turn, direct, move_cols,
     grads, rows_back, send_out,
-    near_sem, table_sem, own_sem, in_s, in_r, mg_ss, mg_r, t1_s, t1_r, t2_s, t2_r, kb_s, kb_r, gb_s, gb_r, out_s, out_r,
+    near_sem, table_sem, sent, in_r, mg_r, t1_r, t2_r, kb_r, gb_r, out_r,
 ):
     Dt, Dm, B, Bl, ml, M, A, Al, As, Ak, J, total = sizes
     parts = 2 if Ak % 16 == 0 else 1
@@ -177,20 +177,14 @@
         staged[-1].start()
     pl.semaphore_wait(barrier, Dt + Dm - 2)
 
-    sends = []
-    owns = {}
-    own_count = [0]
-
-    def go(src, dst, send, recv, axis, peer):
-        copy = remote(src, dst, send, recv, axis, peer)
-        copy.start()
-        sends.append(copy)
-
-    def own(name, src, dst):
-        copy = pltpu.make_async_copy(src, dst, own_sem.at[own_count[0]])
-        own_count[0] += 1
-        copy.start()
-        owns[name] = copy
+    def go(src, dst, leg, recv, axis, peer):
+        remote(src, dst, sent.at[leg], recv, axis, peer).start()
+
+    def own(src, dst, recv):
+        pltpu.make_async_copy(src, dst, recv).start()
+
+    def arrived(whole, recv):
+        pltpu.make_async_copy(whole, whole, recv).wait()
 
     def target_part(i, b):
         if (As * ml) % 8 == 0:
@@ -199,28 +193,26 @@
 
     def target_first_leg(b):
         for peer in mode_peers:
-            go(target_part(peer, b), t1[b].at[me_m], t1_s.at[b, peer], t1_r.at[b, me_m], "mode", peer)
-        own(("t1", b), target_part(me_m, b), t1[b].at[me_m])
+            go(target_part(peer, b), t1.at[b, me_m], 2, t1_r.at[b], "mode", peer)
+        own(target_part(me_m, b), t1.at[b, me_m], t1_r.at[b])
 
     def target_second_leg(b):
-        owns[("t1", b)].wait()
-        for peer in mode_peers:
-            remote(target_part(0, b), t1[b].at[peer], t1_s.at[b, peer], t1_r.at[b, peer], "mode", peer).wait_recv()
+        arrived(t1.at[b], t1_r.at[b])
         for peer in tm_peers:
-            go(t1[b].at[:, :, peer], t2[b].at[me_t], t2_s.at[b, peer], t2_r.at[b, me_t], "tm", peer)
-        own(("t2", b), t1[b].at[:, :, me_t], t2[b].at[me_t])
+            go(t1.at[b, :, :, peer], t2.at[b, me_t], 3, t2_r.at[b], "tm", peer)
+        own(t1.at[b, :, :, me_t], t2.at[b, me_t], t2_r.at[b])
 
     staged[0].wait()
     for peer in mode_peers:
-        go(margin, mg.at[me_m], mg_ss.at[peer], mg_r.at[me_m], "mode", peer)
-    own("mg", margin, mg.at[me_m])
+        go(margin, mg.at[me_m], 1, mg_r, "mode", peer)
+    own(margin, mg.at[me_m], mg_r)
     staged[1].wait()
     target_first_leg(0)
     staged[2].wait()
     for b in range(Bl):
         for peer in tm_peers:
-            go(x_near.at[:, peer * Bl + b], rows_in.at[b, me_t], in_s.at[b, peer], in_r.at[b, me_t], "tm", peer)
-        own(("in", b), x_near.at[:, me_t * Bl + b], rows_in.at[b, me_t])
+            go(x_near.at[:, peer * Bl + b], rows_in.at[b, me_t], 0, in_r.at[b], "tm", peer)
+        own(x_near.at[:, me_t * Bl + b], rows_in.at[b, me_t], in_r.at[b])
     for b in range(1, Bl):
         target_first_leg(b)
     for copy in staged[3:]:
@@ -279,7 +271,7 @@
         rows = pl.ds(h * Hk, Hk)
         go(
             grads.at[b, peer * ml + m, :, rows], rows_back.at[b, m, me_m, :, rows],
-            gb_s.at[b, h, m, peer], gb_r.at[b, h, m, me_m], "mode", peer,
+            5, gb_r.at[b, m], "mode", peer,
         )
 
     def line_up(b):
@@ -288,45 +280,58 @@
             owner, local = p // ml, lax.rem(p, ml)
             for ri in range(2):
                 wanted[p, ri] = jnp.concatenate(
-                    [t2[b][j, owner, ri, pl.ds(local, As, stride=ml), :] for j in range(Dt)], axis=0
+                    [t2[b, j, owner, ri, pl.ds(local, As, stride=ml), :] for j in range(Dt)], axis=0
                 )
+
+    def each(count, body):
+        if M <= 8:
+            for i in range(count):
+                body(i)
+        else:
+            pl.loop(0, count)(body)
+
+    def span(start, size):
+        return pl.ds(start if isinstance(start, int) else pl.multiple_of(start, size), size)
 
     def kerr(b, h):
         field = kb[b * parts + h]
         tiles = Hk // 8
         depth = J * 8
 
-        for j in range(0, J, 2):
-            made = []
-            for s in range(2):
-                first, second = pairs[0, j + s], pairs[1, j + s]
-                ar, ai = field[first, 0], field[first, 1]
-                br, bi = field[second, 0], field[second, 1]
-                made.append((ar * br - ai * bi, ar * bi + ai * br))
-            for q in range(tiles):
+        def block(ref, row, q):
+            return [ref[span(row * 8, 8), (2 * q + ri) * 128 : (2 * q + ri + 1) * 128] for ri in range(2)]
+
+        def put(ref, start, q, ri, value):
+            ref[span(start, 16), (2 * q + ri) * 128 : (2 * q + ri + 1) * 128] = value
+
+        def multiply_pairs(q):
+            here = pl.ds(q * 8, 8)
+            for j in range(0, J, 2):
+                made = []
+                for s in range(2):
+                    first, second = pairs[0, j + s], pairs[1, j + s]
+                    ar, ai = field[first, 0, here], field[first, 1, here]
+                    br, bi = field[second, 0, here], field[second, 1, here]
+                    made.append((ar * br - ai * bi, ar * bi + ai * br))
                 for ri in range(2):
-                    high, low = halves(
-                        jnp.concatenate([made[s][ri][q * 8 : q * 8 + 8] for s in range(2)], axis=0)
-                    )
-                    cols = pl.ds((2 * q + ri) * 128, 128)
-                    pair_cols[j * 8 : j * 8 + 16, cols] = high
-                    pair_cols[depth + j * 8 : depth + j * 8 + 16, cols] = low
-                    pair_cols[2 * depth + j * 8 : 2 * depth + j * 8 + 16, cols] = high
-        for q in range(tiles):
+                    high, low = halves(jnp.concatenate([value[ri] for value in made], axis=0))
+                    for part, value in enumerate((high, low, high)):
+                        put(pair_cols, part * depth + j * 8, q, ri, value)
+
+        def couple(q):
             cols = pl.ds(q * 256, 256)
             coup[:, cols] = mm(w1[...], pair_cols[:, cols])
 
-        @pl.loop(0, M // 2)
-        def _(pp):
-            for q in range(tiles):
-                rows, here = pl.ds(h * Hk + q * 8, 8), pl.ds(q * 8, 8)
+        def compare(q):
+            rows, here = pl.ds(h * Hk + q * 8, 8), pl.ds(q * 8, 8)
+
+            def body(pp):
                 pushed = []
                 for s in range(2):
                     p = pp * 2 + s
                     kr = ki = jnp.zeros((8, 128), f32)
                     for n in range(M):
-                        at = pl.ds(pl.multiple_of((p * M + n) * 8, 8), 8)
-                        cr, ci = coup[at, q * 256 : q * 256 + 128], coup[at, q * 256 + 128 : q * 256 + 256]
+                        cr, ci = block(coup, p * M + n, q)
                         ur, ui = field[n, 0, here], field[n, 1, here]
                         kr = kr + (cr * ur + ci * ui)
                         ki = ki + (ci * ur - cr * ui)
@@ -338,70 +343,79 @@
                     push[p, 0, rows] = pushed[s][0]
                     push[p, 1, rows] = pushed[s][1]
                 for ri in range(2):
-                    high, low = halves(jnp.concatenate([pushed[s][ri] for s in range(2)], axis=0))
-                    cols = pl.ds((2 * q + ri) * 128, 128)
+                    high, low = halves(jnp.concatenate([value[ri] for value in pushed], axis=0))
                     for part, value in enumerate((high, low, high)):
-                        push_cols[pl.ds(pl.multiple_of(part * (M * 8) + pp * 16, 16), 16), cols] = value
-
-        for q in range(tiles):
+                        put(push_cols, part * (M * 8) + pp * 16, q, ri, value)
+
+            each(M // 2, body)
+
+        def turn_back(q):
             cols = pl.ds(q * 256, 256)
             turn[:, cols] = mm(w2[...], push_cols[:, cols])
 
-        @pl.loop(0, M)
-        def _(n):
-            for q in range(tiles):
-                rows, here = pl.ds(h * Hk + q * 8, 8), pl.ds(q * 8, 8)
+        def through_conjugate(q):
+            rows = pl.ds(h * Hk + q * 8, 8)
+
+            def body(n):
                 gr, gi = cots[n, 0, rows], cots[n, 1, rows]
                 for p in range(M):
-                    at = pl.ds(pl.multiple_of((p * M + n) * 8, 8), 8)
-                    cr, ci = coup[at, q * 256 : q * 256 + 128], coup[at, q * 256 + 128 : q * 256 + 256]
+                    cr, ci = block(coup, p * M + n, q)
                     er, ei = push[p, 0, rows], push[p, 1, rows]
                     gr = gr + (er * cr + ei * ci)
                     gi = gi + (er * ci - ei * cr)
-                cots[n, 0, rows] = gr
-                cots[n, 1, rows] = gi
-
-        @pl.loop(0, J // 2)
-        def _(jj):
-            for q in range(tiles):
-                rows, here = pl.ds(h * Hk + q * 8, 8), pl.ds(q * 8, 8)
-                moved = []
+                direct[n, 0, rows] = gr
+                direct[n, 1, rows] = gi
+
+            each(M, body)
+
+        def through_pairs(q):
+            here = pl.ds(q * 8, 8)
+
+            def body(jj):
+                moved = [[], []]
                 for s in range(2):
                     j = jj * 2 + s
                     gr = gi = jnp.zeros((8, 128), f32)
                     for n in range(M):
-                        at = pl.ds(pl.multiple_of((n * J + j) * 8, 8), 8)
-                        tr, ti = turn[at, q * 256 : q * 256 + 128], turn[at, q * 256 + 128 : q * 256 + 256]
+                        tr, ti = block(turn, n * J + j, q)
                         ur, ui = field[n, 0, here], field[n, 1, here]
                         gr = gr + (tr * ur - ti * ui)
                         gi = gi + (tr * ui + ti * ur)
                     for side in range(2):
                         other = pairs[1 - side, j]
                         vr, vi = field[other, 0, here], field[other, 1, here]
-                        moved.append((side, (vr * gr + vi * gi, vr * gi - vi * gr)))
+                        moved[side].append((vr * gr + vi * gi, vr * gi - vi * gr))
                 for side in range(2):
                     for ri in range(2):
-                        high, low = halves(
-                            jnp.concatenate([value[ri] for which, value in moved if which == side], axis=0)
-                        )
-                        cols = pl.ds((2 * q + ri) * 128, 128)
-                        at = side * depth + jj * 16
-                        move_cols[pl.ds(pl.multiple_of(at, 16), 16), cols] = high
-                        move_cols[pl.ds(pl.multiple_of(2 * depth + at, 16), 16), cols] = low
-
-        for q in range(tiles):
+                        high, low = halves(jnp.concatenate([value[ri] for value in moved[side]], axis=0))
+                        put(move_cols, side * depth + jj * 16, q, ri, high)
+                        put(move_cols, (2 + side) * depth + jj * 16, q, ri, low)
+
+            each(J // 2, body)
+
+        def gather(q):
             rows = pl.ds(h * Hk + q * 8, 8)
             back = mm(spread[...], move_cols[:, q * 256 : q * 256 + 256])
             for n in range(M):
                 for ri in range(2):
                     grads[b, n, ri, rows] = (
-                        cots[n, ri, rows] + back[n * 8 : n * 8 + 8, ri * 128 : ri * 128 + 128]
+                        direct[n, ri, rows] + back[n * 8 : n * 8 + 8, ri * 128 : ri * 128 + 128]
                     )
 
+        for q in range(tiles):
+            multiply_pairs(q)
+        for q in range(tiles):
+            couple(q)
+        for q in range(tiles):
+            compare(q)
+            turn_back(q)
+        for q in range(tiles):
+            through_conjugate(q)
+            through_pairs(q)
+            gather(q)
+
     for b in range(Bl):
-        owns[("in", b)].wait()
-        for peer in tm_peers:
-            remote(x_near.at[:, b], rows_in.at[b, peer], in_s.at[b, peer], in_r.at[b, peer], "tm", peer).wait_recv()
+        arrived(rows_in.at[b], in_r.at[b])
         stacked = jnp.concatenate(
             [
                 jnp.concatenate(
@@ -423,31 +437,22 @@
             for peer in mode_peers:
                 go(
                     send_z.at[peer, b, h], kb[b * parts + h].at[pl.ds(me_m * ml, ml)],
-                    kb_s.at[b, h, peer], kb_r.at[b, h, me_m], "mode", peer,
+                    4, kb_r.at[b, h], "mode", peer,
                 )
-            own(("kb", b, h), send_z.at[me_m, b, h], kb[b * parts + h].at[pl.ds(me_m * ml, ml)])
+            own(send_z.at[me_m, b, h], kb[b * parts + h].at[pl.ds(me_m * ml, ml)], kb_r.at[b, h])
         if b == 0:
             target_second_leg(0)
 
-    owns["mg"].wait()
-    for peer in mode_peers:
-        remote(margin, mg.at[peer], mg_ss.at[peer], mg_r.at[peer], "mode", peer).wait_recv()
+    arrived(mg, mg_r)
     make_weights(sizes, pairs, mg, w1, w2, spread)
     for b in range(1, Bl):
         target_second_leg(b)
 
     for b in range(Bl):
-        owns[("t2", b)].wait()
-        for peer in tm_peers:
-            remote(t1[b].at[:, :, 0], t2[b].at[peer], t2_s.at[b, peer], t2_r.at[b, peer], "tm", peer).wait_recv()
+        arrived(t2.at[b], t2_r.at[b])
         line_up(b)
         for h in range(parts):
-            owns[("kb", b, h)].wait()
-            for peer in mode_peers:
-                remote(
-                    send_z.at[0, b, h], kb[b * parts + h].at[pl.ds(peer * ml, ml)],
-                    kb_s.at[b, h, peer], kb_r.at[b, h, peer], "mode", peer,
-                ).wait_recv()
+            arrived(kb[b * parts + h], kb_r.at[b, h])
             kerr(b, h)
             if b + 1 < Bl:
                 for m in range(ml):
@@ -459,18 +464,11 @@
                     for h in range(parts):
                         send_gradient(b, h, m, peer)
         for m in range(ml):
-            own(("gb", b, m), grads.at[b, me_m * ml + m], rows_back.at[b, m, me_m])
+            own(grads.at[b, me_m * ml + m], rows_back.at[b, m, me_m], gb_r.at[b, m])
 
     for b in range(Bl):
         for m in range(ml):
-            owns[("gb", b, m)].wait()
-            for peer in mode_peers:
-                for h in range(parts):
-                    rows = pl.ds(h * Hk, Hk)
-                    remote(
-                        grads.at[b, m, :, rows], rows_back.at[b, m, peer, :, rows],
-                        gb_s.at[b, h, m, peer], gb_r.at[b, h, m, peer], "mode", peer,
-                    ).wait_recv()
+            arrived(rows_back.at[b, m], gb_r.at[b, m])
             stacked = jnp.concatenate(
                 [
                     rows_back[b, m, i, ri, j * As : (j + 1) * As, :]
@@ -488,33 +486,31 @@
             for peer in tm_peers:
                 go(
                     send_out.at[peer, b, m], out.at[:, me_t * Bl + b, m],
-                    out_s.at[b, m, peer], out_r.at[b, m, me_t], "tm", peer,
+                    6, out_r, "tm", peer,
                 )
-            own(("out", b, m), send_out.at[me_t, b, m], out.at[:, me_t * Bl + b, m])
-    for b in range(Bl):
+            own(send_out.at[me_t, b, m], out.at[:, me_t * Bl + b, m], out_r)
+    arrived(out, out_r)
+    others_t, others_m = pl.ds(0, Dt - 1), pl.ds(0, Dm - 1)
+    for leg, whole in enumerate(
+        (
+            rows_in.at[:, others_t],
+            mg.at[others_m],
+            t1.at[:, others_m],
+            t2.at[:, others_t],
+            send_z.at[others_m],
+            rows_back.at[:, :, others_m],
+            send_out.at[others_t],
+        )
+    ):
+        arrived(whole, sent.at[leg])
+
+
+def finish(gathered, out, sem):
+    _, B, ml, _, _ = gathered.shape
+    for b in range(B):
         for m in range(ml):
-            owns[("out", b, m)].wait()
-            for peer in tm_peers:
-                remote(
-                    send_out.at[0, b, m], out.at[:, peer * Bl + b, m],
-                    out_s.at[b, m, peer], out_r.at[b, m, peer], "tm", peer,
-                ).wait_recv()
-    for copy in sends:
-        copy.wait_send()
-
-
-def finish(gathered, out, woven, sem):
-    _, B, ml, Al, _ = gathered.shape
-    copies = []
-    for b in range(B):
-        for ri in range(2):
-            for m in range(ml):
-                woven[ri, b, pl.ds(m, Al, stride=ml), :] = gathered[ri, b, m]
-        copy = pltpu.make_async_copy(woven.at[:, b], out.at[:, b], sem.at[b])
-        copy.start()
-        copies.append(copy)
-    for copy in copies:
-        copy.wait()
+            pltpu.make_async_copy(gathered.at[:, b, m], out.at[:, b, :, m], sem).start()
+    pltpu.make_async_copy(gathered, gathered, sem).wait()
 
 
 def on_device(Dm, Dt, input_field, target_field, margin, pair_index, mode_beta, segment_kind):
@@ -541,12 +537,11 @@
     vb = lambda *shape: pltpu.VMEM(shape, bf16)
     dma = lambda *shape: pltpu.SemaphoreType.DMA(shape)
     anyspace = pl.BlockSpec(memory_space=pl.ANY)
-    vmem = pl.BlockSpec(memory_space=pltpu.VMEM)
     gathered = pl.pallas_call(
         functools.partial(kernel, sizes),
         out_shape=pltpu.VMEM((2, B, ml, Al, 128), f32),
         in_specs=[anyspace] * 11,
-        out_specs=vmem,
+        out_specs=anyspace,
         scratch_shapes=[
             vm(*x.shape),
             vm(*target.shape),
@@ -562,8 +557,8 @@
             vm(Bl, Dt, 2, Al * ml, 128),
             vm(Dm, Bl, parts, ml, 2, Hk, 128),
             [vm(M, 2, Hk, 128) for _ in range(Bl * parts)],
-            [vm(Dm, 2, Dt, As * ml, 128) for _ in range(Bl)],
-            [vm(Dt, Dm, 2, As * ml, 128) for _ in range(Bl)],
+            vm(Bl, Dm, 2, Dt, As * ml, 128),
+            vm(Bl, Dt, Dm, 2, As * ml, 128),
             vm(Dm, ml, M, J),
             vb(M * M * 8, 3 * J * 8),
             vb(M * J * 8, 3 * M * 8),
@@ -575,31 +570,32 @@
             vm(M, 2, Ak, 128),
             vb(3 * M * 8, Hk * 32),
             vm(M * J * 8, Hk * 32),
+            vm(M, 2, Ak, 128),
             vb(4 * J * 8, Hk * 32),
             vm(Bl, M, 2, Ak, 128),
             vm(Bl, ml, Dm, 2, Ak, 128),
             vm(Dt, Bl, ml, 2, Al, 128),
             dma(5),
             dma(6),
-            dma((3 + parts + 2 * ml) * Bl + 1),
-            dma(Bl, Dt), dma(Bl, Dt),
-            dma(Dm), dma(Dm),
-            dma(Bl, Dm), dma(Bl, Dm),
-            dma(Bl, Dt), dma(Bl, Dt),
-            dma(Bl, parts, Dm), dma(Bl, parts, Dm),
-            dma(Bl, parts, ml, Dm), dma(Bl, parts, ml, Dm),
-            dma(Bl, ml, Dt), dma(Bl, ml, Dt),
+            dma(7),
+            dma(Bl),
+            dma(),
+            dma(Bl),
+            dma(Bl),
+            dma(Bl, parts),
+            dma(Bl, ml),
+            dma(),
         ],
         compiler_params=pltpu.CompilerParams(collective_id=0, has_side_effects=True, vmem_limit_bytes=62 * 1024 * 1024),
     )(segment_kind, pair_index.T, x, target, margin, mode_beta.transpose(2, 1, 0), *[jnp.asarray(t) for t in tables])
     out = pl.pallas_call(
         finish,
-        out_shape=jax.ShapeDtypeStruct((2, B, Al * ml, 128), f32),
-        in_specs=[vmem],
+        out_shape=jax.ShapeDtypeStruct((2, B, Al, ml, 128), f32),
+        in_specs=[anyspace],
         out_specs=anyspace,
-        scratch_shapes=[vm(2, B, Al * ml, 128), dma(B)],
+        scratch_shapes=[dma()],
     )(pltpu.with_memory_space_constraint(gathered, pltpu.VMEM))
-    return out.reshape(2, B, Al, ml, 128).transpose(0, 1, 3, 2, 4).reshape(2, B, ml, Tl)
+    return out.transpose(0, 1, 3, 2, 4).reshape(2, B, ml, Tl)
 
 
 def solution(mesh):

time: 48.6 us -> 46.7 us (0.961)
  Pallas kernels: 47.8 us -> 45.9 us
    pallas_call x1, Pallas kernels: 46.9 us -> 45.1 us  [on_device(): pl.pallas_call(functools.partial(kernel, sizes), out_shape=pltpu.VMEM((2,...]
where the time goes in v4:
time: 46.7 us; the launch traced here: 46.5 us
  Pallas kernels  45.9 us (98%)
  between operations  0.66 us (1%)
    pallas_call x1, Pallas kernels, on_device(): pl.pallas_call(functools.partial(kernel, sizes), out_shape=pltpu.VMEM((2,...  45.1 us

profile of v4, /device:TPU:0, one launch (start us, length us, event | category | flops | bytes accessed | tf_op | source)
XLA Modules:
  0.0 46.5 jit_solution(13098775917154740288)
XLA Ops:
  0.7 45.1 %shard_map.109.gathered = f32[2,8,2,32,128]{4,3,2,1,0:T(8,128)S(1)} custom-call(s32[1]{0:T(128)S(6)} %copy.14.kind_hbm, s32[2,16]{1,0:T(2,128)} %bitcast.18, f32[2,8,64,128]{3,2,1,0:T(8,128)} %bitcast.15, f32[2,4,2,64,128]{4,3,2,1,0:T(8,128)} %bitcast.16, f32[2,8,16]{2,1,0:T(8,128)} %margin_hbm.1, f32[3,2,1024]{2,1,0:T(2,128)} %bitcast.17, ...), custom_call_target="tpu_custom_call" | custom-call | tf_op jit(solution)/shard_map/pallas_call | solution.py:540
  45.8 0.8 %shard_map.110 = f32[2,8,32,2,128]{4,3,2,1,0:T(2,128)} custom-call(f32[2,8,2,32,128]{4,3,2,1,0:T(8,128)S(1)} %shard_map.109.gathered), custom_call_target="tpu_custom_call" | custom-call | tf_op jit(solution)/shard_map/pallas_call | solution.py:591

commit v5 on v4

--- a/solution.py
+++ b/solution.py
@@ -53,12 +53,18 @@
 
 def left_dot(table, value):
     high, low = halves(value)
-    return mm(table[0], high) + (mm(table[0], low) + mm(table[1], high))
+    width = value.shape[1]
+    if width > 128:
+        return mm(table[0], high) + (mm(table[0], low) + mm(table[1], high))
+    both = mm(table[0], jnp.concatenate([high, low], axis=1))
+    return both[:, :width] + (both[:, width:] + mm(table[1], high))
 
 
 def right_dot(value, table):
     high, low = halves(value)
-    return mm(high, table[0]) + (mm(low, table[0]) + mm(high, table[1]))
+    rows = value.shape[0]
+    both = mm(jnp.concatenate([high, low], axis=0), table[0])
+    return both[:rows] + (both[rows:] + mm(high, table[1]))
 
 
 def farthest_first(me, count):
@@ -434,7 +440,7 @@
                         h, at = j * As // Hk, j * As % Hk
                         send_z[i, b, h, m, ri, at : at + As, :] = result[row : row + As, m * 128 : (m + 1) * 128]
         for h in range(parts):
-            for peer in mode_peers:
+            for peer in mode_peers[::-1]:
                 go(
                     send_z.at[peer, b, h], kb[b * parts + h].at[pl.ds(me_m * ml, ml)],
                     4, kb_r.at[b, h], "mode", peer,

time: 46.7 us -> 45.9 us (0.983)
  Pallas kernels: 45.9 us -> 45.1 us
    pallas_call x1, Pallas kernels: 45.1 us -> 44.3 us  [on_device(): pl.pallas_call(functools.partial(kernel, sizes), out_shape=pltpu.VMEM((2,...]
where the time goes in v5:
time: 45.9 us; the launch traced here: 45.7 us
  Pallas kernels  45.1 us (98%)
  between operations  0.66 us (1%)
    pallas_call x1, Pallas kernels, on_device(): pl.pallas_call(functools.partial(kernel, sizes), out_shape=pltpu.VMEM((2,...  44.3 us

profile of v5, /device:TPU:0, one launch (start us, length us, event | category | flops | bytes accessed | tf_op | source)
XLA Modules:
  0.0 45.7 jit_solution(16916445290263962291)
XLA Ops:
  0.7 44.3 %shard_map.109.gathered = f32[2,8,2,32,128]{4,3,2,1,0:T(8,128)S(1)} custom-call(s32[1]{0:T(128)S(6)} %copy.14.kind_hbm, s32[2,16]{1,0:T(2,128)} %bitcast.18, f32[2,8,64,128]{3,2,1,0:T(8,128)} %bitcast.15, f32[2,4,2,64,128]{4,3,2,1,0:T(8,128)} %bitcast.16, f32[2,8,16]{2,1,0:T(8,128)} %margin_hbm.1, f32[3,2,1024]{2,1,0:T(2,128)} %bitcast.17, ...), custom_call_target="tpu_custom_call" | custom-call | tf_op jit(solution)/shard_map/pallas_call | solution.py:546
  45.0 0.8 %shard_map.110 = f32[2,8,32,2,128]{4,3,2,1,0:T(2,128)} custom-call(f32[2,8,2,32,128]{4,3,2,1,0:T(8,128)S(1)} %shard_map.109.gathered), custom_call_target="tpu_custom_call" | custom-call | tf_op jit(solution)/shard_map/pallas_call | solution.py:597

commit v6 on v5

--- a/solution.py
+++ b/solution.py
@@ -446,12 +446,10 @@
                     4, kb_r.at[b, h], "mode", peer,
                 )
             own(send_z.at[me_m, b, h], kb[b * parts + h].at[pl.ds(me_m * ml, ml)], kb_r.at[b, h])
-        if b == 0:
-            target_second_leg(0)
 
     arrived(mg, mg_r)
     make_weights(sizes, pairs, mg, w1, w2, spread)
-    for b in range(1, Bl):
+    for b in range(Bl):
         target_second_leg(b)
 
     for b in range(Bl):

time: 45.9 us -> 45.9 us (level)
  no operation moved by 1% of the time
where the time goes in v6:
time: 45.9 us; the launch traced here: 45.7 us
  Pallas kernels  45.1 us (98%)
  between operations  0.66 us (1%)
    pallas_call x1, Pallas kernels, on_device(): pl.pallas_call(functools.partial(kernel, sizes), out_shape=pltpu.VMEM((2,...  44.3 us

profile of v6, /device:TPU:0, one launch (start us, length us, event | category | flops | bytes accessed | tf_op | source)
XLA Modules:
  0.0 45.7 jit_solution(13048063454208138749)
XLA Ops:
  0.7 44.3 %shard_map.109.gathered = f32[2,8,2,32,128]{4,3,2,1,0:T(8,128)S(1)} custom-call(s32[1]{0:T(128)S(6)} %copy.14.kind_hbm, s32[2,16]{1,0:T(2,128)} %bitcast.18, f32[2,8,64,128]{3,2,1,0:T(8,128)} %bitcast.15, f32[2,4,2,64,128]{4,3,2,1,0:T(8,128)} %bitcast.16, f32[2,8,16]{2,1,0:T(8,128)} %margin_hbm.1, f32[3,2,1024]{2,1,0:T(2,128)} %bitcast.17, ...), custom_call_target="tpu_custom_call" | custom-call | tf_op jit(solution)/shard_map/pallas_call | solution.py:544
  45.0 0.8 %shard_map.110 = f32[2,8,32,2,128]{4,3,2,1,0:T(2,128)} custom-call(f32[2,8,2,32,128]{4,3,2,1,0:T(8,128)S(1)} %shard_map.109.gathered), custom_call_target="tpu_custom_call" | custom-call | tf_op jit(solution)/shard_map/pallas_call | solution.py:595
